TPU v7x, 128 devices: a whole 4x4x4 slice. The times are simulated.
128 devices in a mesh: tile: 32 (over x, y, core), head: 4 (over z).
Axes of the slice: x: 4, y: 4, z: 4, core: 2. Of those that a mesh axis runs over, the one named last changes fastest.
Arguments:
- latent: bfloat16 [64, 512, 512], P('tile', 'head'), may hold values from -6 to 6
- norm1_gain: float32 [512], replicated, may hold values from 0.25 to 1.75
- norm1_shift: float32 [512], replicated, may hold values from -1.75 to 1.75
- conv1_weight: bfloat16 [3, 3, 512, 512], replicated, may hold values from -0.09375 to 0.09375
- conv1_bias: float32 [512], replicated, may hold values from -1.75 to 1.75
- norm2_gain: float32 [512], replicated, may hold values from 0.25 to 1.75
- norm2_shift: float32 [512], replicated, may hold values from -1.75 to 1.75
- conv2_weight: bfloat16 [3, 3, 512, 512], replicated, may hold values from -0.09375 to 0.09375
- conv2_bias: float32 [512], replicated, may hold values from -1.75 to 1.75
- norm3_gain: float32 [512], replicated, may hold values from 0.25 to 1.75
- norm3_shift: float32 [512], replicated, may hold values from -1.75 to 1.75
- query_weight: bfloat16 [512, 512], replicated, may hold values from -2 to 2
- query_bias: float32 [512], replicated, may hold values from -3 to 3
- key_weight: bfloat16 [512, 512], replicated, may hold values from -2 to 2
- value_weight: bfloat16 [512, 512], replicated, may hold values from -0.25 to 0.25
- value_bias: float32 [512], replicated, may hold values from -3 to 3
- out_weight: bfloat16 [512, 512], replicated, may hold values from -0.5 to 0.5
- out_bias: float32 [512], replicated, may hold values from -1.75 to 1.75
Outputs:
- block_out: bfloat16 [64, 512, 512], P('tile', 'head')
All inputs are finite; a program needn't handle non-finite values.
Results may differ from a plain program's by a relative error of at most 0.01615.
Values may be sent and summed in bfloat16 or wider, within the bound.
A program may use at most 128 MiB of HBM per device.

v0:
```python
import functools

import jax
import jax.numpy as jnp
from jax import lax
from jax.sharding import Mesh
from jax.sharding import PartitionSpec as P

C = 512
GROUPS = 32
TILE_HEAD = ("tile_0", "tile_1", "tile_2", "head")
TILE = ("tile_0", "tile_1", "tile_2")


def over_axes(x, axes):
    return functools.reduce(lax.psum, axes, x)


def extended(x, sides, width):
    for axis, dim in sides:
        peers, length = (lax.axis_size(axis), x.shape[dim])
        up = [(i, (i + 1) % peers) for i in range(peers - 1)]
        down = [(j, i) for i, j in up]
        last = lax.slice_in_dim(x, length - width, length, axis=dim)
        initial = lax.slice_in_dim(x, 0, width, axis=dim)
        before = lax.ppermute(last, axis, up)
        after = lax.ppermute(initial, axis, down)
        x = jnp.concatenate([before, x, after], axis=dim)
    return x


def joined_along(blocks, dim):
    blocks = jnp.moveaxis(blocks, 0, dim)
    dims = blocks.shape
    return blocks.reshape(*dims[:dim], dims[dim] * dims[dim + 1], *dims[dim + 2 :])


def sent_to_all(x, axis):
    peers = lax.axis_size(axis)
    return lax.all_to_all(jnp.broadcast_to(x[None], (peers, *x.shape)), axis, 0, 0, tiled=True)


def gather_directly(x, axis, dim):
    return joined_along(sent_to_all(x, axis), dim)


def side_by_side(arrays, axis, dim, along):
    ends, at = ([], 0)
    for a in arrays[:-1]:
        at += a.shape[along]
        ends.append(at)
    both = jnp.concatenate(arrays, axis=along)
    return tuple(jnp.split(lax.all_gather(both, axis, axis=dim, tiled=True), ends, axis=along))


def of_everyone(x, axis):
    everything = sent_to_all(x, axis)
    return jnp.max(everything, axis=0)


def in_blocks(x, dim, peers):
    before, after = (x.shape[:dim], x.shape[dim + 1 :])
    return jnp.moveaxis(x.reshape(*before, peers, -1, *after), dim, 0)


def sent_and_summed(x, axis, dim):
    peers = lax.axis_size(axis)
    blocks = lax.all_to_all(in_blocks(x, dim, peers), axis, 0, 0, tiled=True)
    return jnp.sum(blocks.astype(jnp.float32), axis=0)


def in_one_piece(arrays, axis, dim, along):
    columns = [a.reshape(*a.shape[:along], -1) for a in arrays]
    both = jnp.concatenate(columns, axis=along)
    out, at, finished = (sent_and_summed(both, axis, dim), 0, [])
    for a, column in zip(arrays, columns):
        section = out[..., at : at + column.shape[along]]
        finished.append(section.reshape(*section.shape[:along], *a.shape[along:]))
        at += column.shape[along]
    return tuple(finished)


def group_norm(values, gain, shift, members):
    grouped = values.reshape(-1, GROUPS, C // GROUPS)
    sums, squares = (
        over_axes(jnp.sum(grouped, axis=(0, 2)), TILE_HEAD),
        over_axes(jnp.sum(grouped * grouped, axis=(0, 2)), TILE_HEAD),
    )
    mean = sums / members
    variance = squares / members - mean * mean
    deviation = grouped - mean[None, :, None]
    normalized = deviation * lax.rsqrt(variance + 1e-06)[None, :, None]
    return normalized.reshape(values.shape) * gain + shift


def conv_three(act, weight, bias):
    padded = extended(act, ((TILE, 0), ("head", 1)), 1)
    result = lax.conv_general_dilated(
        padded[None],
        weight,
        (1, 1),
        "VALID",
        dimension_numbers=("NHWC", "HWIO", "NHWC"),
        preferred_element_type=jnp.float32,
    )[0]
    return result + bias


def per_device(
    latent,
    norm1_gain,
    norm1_shift,
    conv1_weight,
    conv1_bias,
    norm2_gain,
    norm2_shift,
    conv2_weight,
    conv2_bias,
    norm3_gain,
    norm3_shift,
    query_weight,
    query_bias,
    key_weight,
    value_weight,
    value_bias,
    out_weight,
    out_bias,
):
    local_rows, local_cols, channels = latent.shape
    positions = local_rows * local_cols
    members = positions * lax.axis_size(TILE) * lax.axis_size("head") * (C // GROUPS)
    latent32 = latent.astype(jnp.float32).reshape(positions, C)
    act1 = jax.nn.silu(group_norm(latent32, norm1_gain, norm1_shift, members)).astype(jnp.bfloat16)
    hidden = conv_three(act1.reshape(local_rows, local_cols, C), conv1_weight, conv1_bias).reshape(
        positions, C
    )
    act2 = jax.nn.silu(group_norm(hidden, norm2_gain, norm2_shift, members)).astype(jnp.bfloat16)
    second = conv_three(act2.reshape(local_rows, local_cols, C), conv2_weight, conv2_bias).reshape(
        positions, C
    )
    resid = (latent32 + second).astype(jnp.bfloat16)
    normed = group_norm(resid.astype(jnp.float32), norm3_gain, norm3_shift, members).astype(
        jnp.bfloat16
    )
    queries = (
        jnp.dot(normed, query_weight, preferred_element_type=jnp.float32) + query_bias
    ).astype(jnp.bfloat16)
    tile_queries = gather_directly(queries, "head", 0)
    query_rows = tile_queries.shape[0]
    softmax_scale = 1.0 / C**0.5
    widest = positions * max(1, 2048 // positions)
    initial = (
        jnp.full((query_rows,), -1e30, jnp.float32),
        jnp.zeros((query_rows,), jnp.float32),
        jnp.zeros((query_rows, C), jnp.float32),
    )
    keys = jnp.dot(normed, key_weight, preferred_element_type=jnp.float32).astype(jnp.bfloat16)
    values = (
        jnp.dot(normed, value_weight, preferred_element_type=jnp.float32) + value_bias
    ).astype(jnp.bfloat16)
    pieces = side_by_side((keys, values), TILE, 0, 1)
    key_rows = pieces[0]
    rows_here = key_rows.shape[0]
    block_len = min(rows_here, widest)
    while rows_here % block_len != 0:
        block_len = block_len - positions
    nblocks = rows_here // block_len

    def step_block(state_in, block_pair):
        run_max, run_sum, weighted = state_in
        key_block, value_block = block_pair
        scores = (
            jnp.dot(tile_queries, key_block.T, preferred_element_type=jnp.float32) * softmax_scale
        )
        new_max = jnp.maximum(run_max, jnp.max(scores, axis=1))
        factor = jnp.exp(run_max - new_max)
        expo = jnp.exp(scores - new_max[:, None])
        run_sum = run_sum * factor + jnp.sum(expo, axis=1)
        weighted = weighted * factor[:, None] + jnp.dot(
            expo.astype(jnp.bfloat16), value_block, preferred_element_type=jnp.float32
        )
        return ((new_max, run_sum, weighted), None)

    blocked = (key_rows.reshape(nblocks, block_len, C), pieces[1].reshape(nblocks, block_len, C))
    state_out, unused = lax.scan(step_block, initial, blocked)
    run_max, run_sum, weighted = state_out
    top = of_everyone(run_max, "head")
    factor = jnp.exp(run_max - top)
    own_weighted, own_sum = in_one_piece(
        (
            (weighted * factor[:, None]).astype(jnp.bfloat16),
            (run_sum * factor).astype(jnp.bfloat16),
        ),
        "head",
        0,
        1,
    )
    attended = (own_weighted / own_sum[:, None]).astype(jnp.bfloat16)
    mixed = (
        resid.astype(jnp.float32)
        + jnp.dot(attended, out_weight, preferred_element_type=jnp.float32)
        + out_bias
    )
    return mixed.astype(jnp.bfloat16).reshape(local_rows, local_cols, C)


def solution(mesh):
    finer = Mesh(
        mesh.devices.reshape(4, 4, 2, mesh.shape["head"]), ("tile_0", "tile_1", "tile_2", "head")
    )
    return jax.shard_map(
        per_device,
        mesh=finer,
        in_specs=(
            P(TILE, "head", None),
            P(),
            P(),
            P(),
            P(),
            P(),
            P(),
            P(),
            P(),
            P(),
            P(),
            P(),
            P(),
            P(),
            P(),
            P(),
            P(),
            P(),
        ),
        out_specs=P(TILE, "head", None),
        check_vma=False,
    )
```

profile of v0, /device:TPU:1, one launch (start us, length us, event | category | flops | bytes accessed | tf_op | source)
XLA Modules:
  0.0 301.4 jit_solution(632631362085679462)
XLA Ops:
  6.5 1.1 convert_reduce_fusion.2
  8.0 9.3 %all-reduce.8 = (f32[32]{0:T(128)S(1)}, f32[32]{0:T(128)S(1)}) all-reduce(f32[32]{0:T(128)S(1)} %reduce_sum.96, f32[32]{0:T(128)S(1)} %reduce_sum.90), channel_id=1, replica_groups=mesh['tile_0'=4,'tile_1'=4,'tile_2'=2,'head'=4] {'tile_0'}, use_global_device_ids=true, to_apply=%region_8.0 | all-reduce | flops 64 | bytes 512 | tf_op jit(solution)/shard_map/psum | solution.py:16
  17.3 9.0 %all-reduce.5 = (f32[32]{0:T(128)S(1)}, f32[32]{0:T(128)S(1)}) all-reduce(f32[32]{0:T(128)S(1)} %get-tuple-element.107, f32[32]{0:T(128)S(1)} %get-tuple-element.108), channel_id=1, replica_groups=mesh['tile_0'=4,'tile_1'=4,'tile_2'=2,'head'=4] {'tile_1'}, use_global_device_ids=true, to_apply=%region_9.0 | all-reduce | flops 64 | bytes 512 | tf_op jit(solution)/shard_map/psum | solution.py:16
  26.3 6.6 %all-reduce.11 = (f32[32]{0:T(128)S(1)}, f32[32]{0:T(128)S(1)}) all-reduce(f32[32]{0:T(128)S(1)} %get-tuple-element.101, f32[32]{0:T(128)S(1)} %get-tuple-element.102), channel_id=1, replica_groups=mesh['tile_0'=4,'tile_1'=4,'tile_2'=2,'head'=4] {'tile_2'}, use_global_device_ids=true, to_apply=%region_10.11 | all-reduce | flops 64 | bytes 512 | tf_op jit(solution)/shard_map/psum | solution.py:16
  32.9 9.7 %all-reduce.2 = (f32[32]{0:T(128)S(1)}, f32[32]{0:T(128)S(1)}) all-reduce(f32[32]{0:T(128)S(1)} %get-tuple-element.113, f32[32]{0:T(128)S(1)} %get-tuple-element.114), channel_id=1, replica_groups=mesh['tile_0'=4,'tile_1'=4,'tile_2'=2,'head'=4] {'head'}, use_global_device_ids=true, to_apply=%region_11.12 | all-reduce | flops 64 | bytes 512 | tf_op jit(solution)/shard_map/psum | solution.py:16
  42.9 1.2 fusion.73
  44.1 3.4 %collective-permute-start = (bf16[1,128,512]{2,1,0:T(8,128)(2,1)S(1)}, bf16[1,128,512]{2,1,0:T(8,128)(2,1)S(1)}, u32[]{:S(2)}, u32[]{:S(2)}) collective-permute-start(bf16[1,128,512]{2,1,0:T(8,128)(2,1)S(1)} %get-tuple-element.129), channel_id=1, source_target_pairs={{0,4},{4,8},{8,12},{12,16},{16,20},{20,24},{24,28},{28,32},{32,36}... | collective-permute-start | bytes 393224 | tf_op jit(solution)/shard_map/ppermute | solution.py:26
  47.5 2.2 collective-permute-start.1
  49.7 1.2 fusion.64
  50.9 2.9 collective-permute-done.1
  53.8 1.6 collective-permute-start.2
  55.4 1.3 collective-permute-start.3
  56.7 3.1 %collective-permute-done.3 = bf16[4,1,512]{2,1,0:T(2,128)(2,1)S(1)} collective-permute-done((bf16[4,1,512]{2,1,0:T(2,128)(2,1)S(1)}, bf16[4,1,512]{2,1,0:T(2,128)(2,1)S(1)}, u32[]{:S(2)}, u32[]{:S(2)}) %collective-permute-start.3) | collective-permute-done | bytes 4128 | tf_op jit(solution)/shard_map/ppermute | solution.py:27
  59.9 0.3 copy.122
  60.2 0.2 pad.clone
  60.6 1.6 select_reduce_fusion.1
  62.6 6.0 %all-reduce.7 = (f32[32]{0:T(128)S(1)}, f32[32]{0:T(128)S(1)}) all-reduce(f32[32]{0:T(128)S(1)} %reduce_sum.125, f32[32]{0:T(128)S(1)} %reduce_sum.100), channel_id=1, replica_groups=mesh['tile_0'=4,'tile_1'=4,'tile_2'=2,'head'=4] {'tile_0'}, use_global_device_ids=true, to_apply=%region_20.21 | all-reduce | flops 64 | bytes 512 | tf_op jit(solution)/shard_map/psum | solution.py:16
  68.6 11.5 %all-reduce.4 = (f32[32]{0:T(128)S(1)}, f32[32]{0:T(128)S(1)}) all-reduce(f32[32]{0:T(128)S(1)} %get-tuple-element.105, f32[32]{0:T(128)S(1)} %get-tuple-element.106), channel_id=1, replica_groups=mesh['tile_0'=4,'tile_1'=4,'tile_2'=2,'head'=4] {'tile_1'}, use_global_device_ids=true, to_apply=%region_21.22 | all-reduce | flops 64 | bytes 512 | tf_op jit(solution)/shard_map/psum | solution.py:16
  80.1 3.8 %all-reduce.10 = (f32[32]{0:T(128)S(1)}, f32[32]{0:T(128)S(1)}) all-reduce(f32[32]{0:T(128)S(1)} %get-tuple-element.99, f32[32]{0:T(128)S(1)} %get-tuple-element.100), channel_id=1, replica_groups=mesh['tile_0'=4,'tile_1'=4,'tile_2'=2,'head'=4] {'tile_2'}, use_global_device_ids=true, to_apply=%region_22.23 | all-reduce | flops 64 | bytes 512 | tf_op jit(solution)/shard_map/psum | solution.py:16
  83.9 7.1 %all-reduce.1 = (f32[32]{0:T(128)S(1)}, f32[32]{0:T(128)S(1)}) all-reduce(f32[32]{0:T(128)S(1)} %get-tuple-element.111, f32[32]{0:T(128)S(1)} %get-tuple-element.112), channel_id=1, replica_groups=mesh['tile_0'=4,'tile_1'=4,'tile_2'=2,'head'=4] {'head'}, use_global_device_ids=true, to_apply=%region_23.24 | all-reduce | flops 64 | bytes 512 | tf_op jit(solution)/shard_map/psum | solution.py:16
  91.3 0.4 copy.105
  92.2 5.9 %collective-permute-start.4 = (bf16[1,128,512]{2,1,0:T(8,128)(2,1)S(1)}, bf16[1,128,512]{2,1,0:T(8,128)(2,1)S(1)}, u32[]{:S(2)}, u32[]{:S(2)}) collective-permute-start(bf16[1,128,512]{2,1,0:T(8,128)(2,1)S(1)} %get-tuple-element.127), channel_id=1, source_target_pairs={{0,4},{4,8},{8,12},{12,16},{16,20},{20,24},{24,28},{28,32},{32,36}... | collective-permute-start | bytes 393224 | tf_op jit(solution)/shard_map/ppermute | solution.py:26
  98.1 1.9 collective-permute-start.5
  100.0 0.2 multiply_convert_fusion.1
  100.2 4.1 %collective-permute-done.5 = bf16[1,128,512]{2,1,0:T(8,128)(2,1)S(1)} collective-permute-done((bf16[1,128,512]{2,1,0:T(8,128)(2,1)S(1)}, bf16[1,128,512]{2,1,0:T(8,128)(2,1)S(1)}, u32[]{:S(2)}, u32[]{:S(2)}) %collective-permute-start.5) | collective-permute-done | bytes 131104 | tf_op jit(solution)/shard_map/ppermute | solution.py:27
  104.4 2.2 collective-permute-start.6
  106.6 1.3 collective-permute-start.7
  107.9 3.1 %collective-permute-done.7 = bf16[4,1,512]{2,1,0:T(2,128)(2,1)S(1)} collective-permute-done((bf16[4,1,512]{2,1,0:T(2,128)(2,1)S(1)}, bf16[4,1,512]{2,1,0:T(2,128)(2,1)S(1)}, u32[]{:S(2)}, u32[]{:S(2)}) %collective-permute-start.7) | collective-permute-done | bytes 4128 | tf_op jit(solution)/shard_map/ppermute | solution.py:27
  111.2 0.3 copy.123
  111.4 0.2 pad.2.clone
  111.8 3.8 %convolution_select_fusion = f32[2,8,17,512]{3,1,2,0:T(8,128)S(1)} fusion(bf16[3,3,512,512]{3,2,1,0:T(8,128)(2,1)} %param.27, bf16[4,1,7,2,512]{4,2,3,0,1:T(8,128)(2,1)S(1)} %slice.66, bf16[4,1,8,17,512]{4,2,3,0,1:T(8,128)(2,1)S(1)} %copy.109, pred[8,17]{0,1:T(8,128)(4,1)S(1)} %copy-done.16), kind=kOutput, calls=%fused_computation.31 | convolution fusion | flops 1285464064 | bytes 5890184 | tf_op jit(solution)/shard_map/conv_general_dilated | solution.py:98
  115.6 0.4 copy.110
  116.3 0.3 copy-done.2
  117.2 6.2 %all-reduce.6 = (f32[32]{0:T(128)S(1)}, f32[32]{0:T(128)S(1)}) all-reduce(f32[32]{0:T(128)S(1)} %reduce_sum.131, f32[32]{0:T(128)S(1)} %reduce_sum.128), channel_id=1, replica_groups=mesh['tile_0'=4,'tile_1'=4,'tile_2'=2,'head'=4] {'tile_0'}, use_global_device_ids=true, to_apply=%region_32.33 | all-reduce | flops 64 | bytes 512 | tf_op jit(solution)/shard_map/psum | solution.py:16
  123.4 9.0 %all-reduce.3 = (f32[32]{0:T(128)S(1)}, f32[32]{0:T(128)S(1)}) all-reduce(f32[32]{0:T(128)S(1)} %get-tuple-element.103, f32[32]{0:T(128)S(1)} %get-tuple-element.104), channel_id=1, replica_groups=mesh['tile_0'=4,'tile_1'=4,'tile_2'=2,'head'=4] {'tile_1'}, use_global_device_ids=true, to_apply=%region_33.34 | all-reduce | flops 64 | bytes 512 | tf_op jit(solution)/shard_map/psum | solution.py:16
  132.4 4.6 %all-reduce.9 = (f32[32]{0:T(128)S(1)}, f32[32]{0:T(128)S(1)}) all-reduce(f32[32]{0:T(128)S(1)} %get-tuple-element.97, f32[32]{0:T(128)S(1)} %get-tuple-element.98), channel_id=1, replica_groups=mesh['tile_0'=4,'tile_1'=4,'tile_2'=2,'head'=4] {'tile_2'}, use_global_device_ids=true, to_apply=%region_34.35 | all-reduce | flops 64 | bytes 512 | tf_op jit(solution)/shard_map/psum | solution.py:16
  137.0 6.1 %all-reduce = (f32[32]{0:T(128)S(1)}, f32[32]{0:T(128)S(1)}) all-reduce(f32[32]{0:T(128)S(1)} %get-tuple-element.109, f32[32]{0:T(128)S(1)} %get-tuple-element.110), channel_id=1, replica_groups=mesh['tile_0'=4,'tile_1'=4,'tile_2'=2,'head'=4] {'head'}, use_global_device_ids=true, to_apply=%region_35.36 | all-reduce | flops 64 | bytes 512 | tf_op jit(solution)/shard_map/psum | solution.py:16
  143.5 0.3 convolution_convert_fusion
  143.8 0.3 fusion.24
  144.1 0.9 pad_maximum_fusion.1
  145.1 0.3 fusion.25
  145.4 1.1 broadcast_in_dim.19
  146.5 4.4 %all-to-all-start = ((bf16[4,256,512]{2,1,0:T(8,128)(2,1)}), bf16[4,256,512]{2,1,0:T(8,128)(2,1)}, u32[]{:S(2)}, u32[]{:S(2)}) async-start(bf16[4,256,512]{2,1,0:T(8,128)(2,1)} %broadcast_in_dim.19), calls=%async_computation | async-start | bytes 2097152 | tf_op jit(solution)/shard_map/all_to_all | solution.py:40
  150.9 65.4 %all-gather.2.cloned.1.call-done = bf16[8192,1024]{1,0:T(8,128)(2,1)} async-done(((bf16[256,1024]{1,0:T(8,128)(2,1)}), bf16[8192,1024]{1,0:T(8,128)(2,1)}) %all-gather.2.cloned.1.call-update) | async-done | bytes 16777232 | tf_op jit(solution)/shard_map/all_gather | solution.py:53
  216.3 11.3 %fusion.86 = (bf16[8192,512]{1,0:T(8,128)(2,1)}, bf16[8192,512]{1,0:T(8,128)(2,1)}) fusion(bf16[8192,1024]{1,0:T(8,128)(2,1)} %all-gather.2.cloned.1.call-done), kind=kLoop, calls=%fused_computation.129 | loop fusion | bytes 33554432 | tf_op jit(solution)/shard_map/split | solution.py:53
  227.6 39.2 %while.15 = (s32[]{:T(128)}, f32[1024]{0:T(1024)S(1)}, f32[1024]{0:T(1024)S(1)}, f32[1024,512]{1,0:T(8,128)S(1)}, bf16[4,2048,512]{2,1,0:T(8,128)(2,1)}, /*index...) while((s32[]{:T(128)}, f32[1024]{0:T(1024)S(1)}, ...), condition=%wide.region_39.40_spmd.clone, body=%wide.region_36.39_spmd.clone.sunk | while | flops 4313322496 | bytes 34668664 | solution.py:185
  227.6 4.2 %multiply_reduce_fusion.2 = (f32[1024]{0:T(1024)S(1)}, f32[2048,1024]{1,0:T(8,128)S(1)}) fusion(bf16[1024,512]{1,0:T(8,128)(2,1)} %get-tuple-element.212, bf16[4,2048,512]{2,1,0:T(8,128)(2,1)} %get-tuple-element.211, s32[]{:T(128)S(6)} %copy.131), kind=kOutput, calls=%fused_computation.1.clone.1 | convolution fusion | flops 2151676928 | bytes 11538436 | tf_op jit(solution)/shard_map/while/body/eval_jaxpr/dot_general | solution.py:173
  231.9 1.4 fusion.103
  233.3 4.1 %fusion.105 = f32[1024,512]{1,0:T(8,128)S(1)} fusion(f32[1024,512]{1,0:T(8,128)S(1)} %get-tuple-element.201, bf16[4,2048,512]{2,1,0:T(8,128)(2,1)} %get-tuple-element.213, s32[]{:T(128)S(6)} %copy.131, f32[2048,1024]{1,0:T(8,128)S(1)} %get-tuple-element.186, f32[1024]{0:T(1024)S(1)} %select_maximum_fusion.2, f32[1024]{0:T(1024)S(1)} %get-tuple-element.188, ...), kind=kOutput, calls=%fused_computation.11.clone.1 | convolution fusion | flops 2155347968 | bytes 14688261 | tf_op jit(solution)/shard_map/while/body/eval_jaxpr/dot_general | solution.py:179
  237.4 4.2 %multiply_reduce_fusion.2 = (f32[1024]{0:T(1024)S(1)}, f32[2048,1024]{1,0:T(8,128)S(1)}) fusion(bf16[1024,512]{1,0:T(8,128)(2,1)} %get-tuple-element.212, bf16[4,2048,512]{2,1,0:T(8,128)(2,1)} %get-tuple-element.211, s32[]{:T(128)S(6)} %copy.131), kind=kOutput, calls=%fused_computation.1.clone.1 | convolution fusion | flops 2151676928 | bytes 11538436 | tf_op jit(solution)/shard_map/while/body/eval_jaxpr/dot_general | solution.py:173
  241.7 1.4 fusion.103
  243.1 4.1 %fusion.105 = f32[1024,512]{1,0:T(8,128)S(1)} fusion(f32[1024,512]{1,0:T(8,128)S(1)} %get-tuple-element.201, bf16[4,2048,512]{2,1,0:T(8,128)(2,1)} %get-tuple-element.213, s32[]{:T(128)S(6)} %copy.131, f32[2048,1024]{1,0:T(8,128)S(1)} %get-tuple-element.186, f32[1024]{0:T(1024)S(1)} %select_maximum_fusion.2, f32[1024]{0:T(1024)S(1)} %get-tuple-element.188, ...), kind=kOutput, calls=%fused_computation.11.clone.1 | convolution fusion | flops 2155347968 | bytes 14688261 | tf_op jit(solution)/shard_map/while/body/eval_jaxpr/dot_general | solution.py:179
  247.2 4.2 %multiply_reduce_fusion.2 = (f32[1024]{0:T(1024)S(1)}, f32[2048,1024]{1,0:T(8,128)S(1)}) fusion(bf16[1024,512]{1,0:T(8,128)(2,1)} %get-tuple-element.212, bf16[4,2048,512]{2,1,0:T(8,128)(2,1)} %get-tuple-element.211, s32[]{:T(128)S(6)} %copy.131), kind=kOutput, calls=%fused_computation.1.clone.1 | convolution fusion | flops 2151676928 | bytes 11538436 | tf_op jit(solution)/shard_map/while/body/eval_jaxpr/dot_general | solution.py:173
  251.5 1.4 fusion.103
  252.9 4.1 %fusion.105 = f32[1024,512]{1,0:T(8,128)S(1)} fusion(f32[1024,512]{1,0:T(8,128)S(1)} %get-tuple-element.201, bf16[4,2048,512]{2,1,0:T(8,128)(2,1)} %get-tuple-element.213, s32[]{:T(128)S(6)} %copy.131, f32[2048,1024]{1,0:T(8,128)S(1)} %get-tuple-element.186, f32[1024]{0:T(1024)S(1)} %select_maximum_fusion.2, f32[1024]{0:T(1024)S(1)} %get-tuple-element.188, ...), kind=kOutput, calls=%fused_computation.11.clone.1 | convolution fusion | flops 2155347968 | bytes 14688261 | tf_op jit(solution)/shard_map/while/body/eval_jaxpr/dot_general | solution.py:179
  257.0 4.2 %multiply_reduce_fusion.2 = (f32[1024]{0:T(1024)S(1)}, f32[2048,1024]{1,0:T(8,128)S(1)}) fusion(bf16[1024,512]{1,0:T(8,128)(2,1)} %get-tuple-element.212, bf16[4,2048,512]{2,1,0:T(8,128)(2,1)} %get-tuple-element.211, s32[]{:T(128)S(6)} %copy.131), kind=kOutput, calls=%fused_computation.1.clone.1 | convolution fusion | flops 2151676928 | bytes 11538436 | tf_op jit(solution)/shard_map/while/body/eval_jaxpr/dot_general | solution.py:173
  261.3 1.4 fusion.103
  262.7 4.1 %fusion.105 = f32[1024,512]{1,0:T(8,128)S(1)} fusion(f32[1024,512]{1,0:T(8,128)S(1)} %get-tuple-element.201, bf16[4,2048,512]{2,1,0:T(8,128)(2,1)} %get-tuple-element.213, s32[]{:T(128)S(6)} %copy.131, f32[2048,1024]{1,0:T(8,128)S(1)} %get-tuple-element.186, f32[1024]{0:T(1024)S(1)} %select_maximum_fusion.2, f32[1024]{0:T(1024)S(1)} %get-tuple-element.188, ...), kind=kOutput, calls=%fused_computation.11.clone.1 | convolution fusion | flops 2155347968 | bytes 14688261 | tf_op jit(solution)/shard_map/while/body/eval_jaxpr/dot_general | solution.py:179
  266.8 8.2 %all_to_all.16 = f32[4,1,1024]{2,1,0:T(1,128)S(1)} all-to-all(f32[4,1,1024]{2,1,0:T(1,128)S(1)} %broadcast_in_dim.20), channel_id=1, replica_groups=mesh['tile_0'=4,'tile_1'=4,'tile_2'=2,'head'=4] {'head'}, dimensions={0} | all-to-all | bytes 32768 | tf_op jit(solution)/shard_map/all_to_all | solution.py:40
  275.0 0.4 concatenate.33
  275.8 0.6 copy.114
  276.5 16.0 %all_to_all.17 = bf16[4,256,513]{1,2,0:T(8,128)(2,1)S(1)} all-to-all(bf16[4,256,513]{1,2,0:T(8,128)(2,1)S(1)} %copy.114), channel_id=1, replica_groups=mesh['tile_0'=4,'tile_1'=4,'tile_2'=2,'head'=4] {'head'}, dimensions={0} | all-to-all | bytes 2101248 | tf_op jit(solution)/shard_map/all_to_all | solution.py:68
  292.9 0.6 copy-done.10
  293.5 1.1 fusion.23
  (107 shorter events, 4.4 us)
Async XLA Ops:
  6.5 136.9 %copy-start = (bf16[512,512]{1,0:T(8,128)(2,1)S(1)}, bf16[512,512]{1,0:T(8,128)(2,1)}, u32[]{:S(2)}) copy-start(bf16[512,512]{1,0:T(8,128)(2,1)} %param.33) | copy-start | bytes 1572868
  6.5 209.8 %all-gather.2.cloned.1.call-start = ((), (), s32[]{:S(2)}) async-start(), calls=%async_computation.3 | async-start | bytes 17301504 | tf_op jit(solution)/shard_map/all_gather | solution.py:53
  44.1 6.7 %collective-permute-start = (bf16[1,128,512]{2,1,0:T(8,128)(2,1)S(1)}, bf16[1,128,512]{2,1,0:T(8,128)(2,1)S(1)}, u32[]{:S(2)}, u32[]{:S(2)}) collective-permute-start(bf16[1,128,512]{2,1,0:T(8,128)(2,1)S(1)} %get-tuple-element.129), channel_id=1, source_target_pairs={{0,4},{4,8},{8,12},{12,16},{16,20},{20,24},{24,28},{28,32},{32,36}... | collective-permute-start | bytes 393224 | tf_op jit(solution)/shard_map/ppermute | solution.py:26
  47.5 6.3 %collective-permute-start.1 = (bf16[1,128,512]{2,1,0:T(8,128)(2,1)S(1)}, bf16[1,128,512]{2,1,0:T(8,128)(2,1)S(1)}, u32[]{:S(2)}, u32[]{:S(2)}) collective-permute-start(bf16[1,128,512]{2,1,0:T(8,128)(2,1)S(1)} %get-tuple-element.130), channel_id=1, source_target_pairs={{4,0},{8,4},{12,8},{16,12},{20,16},{24,20},{28,24},{32,28},{36,32}... | collective-permute-start | bytes 393224 | tf_op jit(solution)/shard_map/ppermute | solution.py:27
  53.8 6.8 %copy-start.7 = (bf16[3,3,512,512]{3,2,1,0:T(8,128)(2,1)S(1)}, bf16[3,3,512,512]{3,2,1,0:T(8,128)(2,1)}, u32[]{:S(2)}) copy-start(bf16[3,3,512,512]{3,2,1,0:T(8,128)(2,1)} %param.23) | copy-start | bytes 14155780
  53.8 2.9 collective-permute-start.2
  55.4 5.2 %copy-start.3 = (f32[512]{0:T(512)S(1)}, f32[512]{0:T(512)}, u32[]{:S(2)}) copy-start(f32[512]{0:T(512)} %param.24) | copy-start | bytes 6148
  55.4 5.2 %copy-start.16 = (pred[8,17]{0,1:T(8,128)(4,1)S(1)}, pred[8,17]{0,1:T(8,128)(4,1)}, u32[]{:S(2)}) copy-start(pred[8,17]{0,1:T(8,128)(4,1)} %constant.49) | copy-start | bytes 412
  55.4 4.4 %collective-permute-start.3 = (bf16[4,1,512]{2,1,0:T(2,128)(2,1)S(1)}, bf16[4,1,512]{2,1,0:T(2,128)(2,1)S(1)}, u32[]{:S(2)}, u32[]{:S(2)}) collective-permute-start(bf16[4,1,512]{2,1,0:T(2,128)(2,1)S(1)} %get-tuple-element.126), channel_id=1, source_target_pairs={{1,0},{2,1},{3,2},{5,4},{6,5},{7,6},{9,8},{10,9},{11,10},{13,12},{... | collective-permute-start | bytes 12296 | tf_op jit(solution)/shard_map/ppermute | solution.py:27
  62.2 29.8 %copy-start.4 = (f32[512]{0:T(512)S(1)}, f32[512]{0:T(512)}, u32[]{:S(2)}) copy-start(f32[512]{0:T(512)} %param.26) | copy-start | bytes 6148
  62.2 29.8 %copy-start.5 = (f32[512]{0:T(512)S(1)}, f32[512]{0:T(512)}, u32[]{:S(2)}) copy-start(f32[512]{0:T(512)} %param.25) | copy-start | bytes 6148
  92.2 8.0 %collective-permute-start.4 = (bf16[1,128,512]{2,1,0:T(8,128)(2,1)S(1)}, bf16[1,128,512]{2,1,0:T(8,128)(2,1)S(1)}, u32[]{:S(2)}, u32[]{:S(2)}) collective-permute-start(bf16[1,128,512]{2,1,0:T(8,128)(2,1)S(1)} %get-tuple-element.127), channel_id=1, source_target_pairs={{0,4},{4,8},{8,12},{12,16},{16,20},{20,24},{24,28},{28,32},{32,36}... | collective-permute-start | bytes 393224 | tf_op jit(solution)/shard_map/ppermute | solution.py:26
  98.1 6.3 %collective-permute-start.5 = (bf16[1,128,512]{2,1,0:T(8,128)(2,1)S(1)}, bf16[1,128,512]{2,1,0:T(8,128)(2,1)S(1)}, u32[]{:S(2)}, u32[]{:S(2)}) collective-permute-start(bf16[1,128,512]{2,1,0:T(8,128)(2,1)S(1)} %get-tuple-element.128), channel_id=1, source_target_pairs={{4,0},{8,4},{12,8},{16,12},{20,16},{24,20},{28,24},{32,28},{36,32}... | collective-permute-start | bytes 393224 | tf_op jit(solution)/shard_map/ppermute | solution.py:27
  104.4 3.5 %collective-permute-start.6 = (bf16[4,1,512]{2,1,0:T(2,128)(2,1)S(1)}, bf16[4,1,512]{2,1,0:T(2,128)(2,1)S(1)}, u32[]{:S(2)}, u32[]{:S(2)}) collective-permute-start(bf16[4,1,512]{2,1,0:T(2,128)(2,1)S(1)} %get-tuple-element.123), channel_id=1, source_target_pairs={{0,1},{1,2},{2,3},{4,5},{5,6},{6,7},{8,9},{9,10},{10,11},{12,13},{... | collective-permute-start | bytes 12296 | tf_op jit(solution)/shard_map/ppermute | solution.py:26
  106.6 4.4 %collective-permute-start.7 = (bf16[4,1,512]{2,1,0:T(2,128)(2,1)S(1)}, bf16[4,1,512]{2,1,0:T(2,128)(2,1)S(1)}, u32[]{:S(2)}, u32[]{:S(2)}) collective-permute-start(bf16[4,1,512]{2,1,0:T(2,128)(2,1)S(1)} %get-tuple-element.124), channel_id=1, source_target_pairs={{1,0},{2,1},{3,2},{5,4},{6,5},{7,6},{9,8},{10,9},{11,10},{13,12},{... | collective-permute-start | bytes 12296 | tf_op jit(solution)/shard_map/ppermute | solution.py:27
  115.6 1.0 copy-start.2
  115.6 0.9 copy-start.6
  116.1 27.3 %copy-start.12 = (f32[512]{0:T(512)S(1)}, f32[512]{0:T(512)}, u32[]{:S(2)}) copy-start(f32[512]{0:T(512)} %param.30) | copy-start | bytes 6148
  116.1 27.3 %copy-start.13 = (f32[512]{0:T(512)S(1)}, f32[512]{0:T(512)}, u32[]{:S(2)}) copy-start(f32[512]{0:T(512)} %param.29) | copy-start | bytes 6148
  116.1 27.6 %copy-start.8 = (bf16[512,512]{1,0:T(8,128)(2,1)S(1)}, bf16[512,512]{1,0:T(8,128)(2,1)}, u32[]{:S(2)}) copy-start(bf16[512,512]{1,0:T(8,128)(2,1)} %param.34) | copy-start | bytes 1572868
  116.2 27.6 %copy-start.11 = (f32[512]{0:T(512)S(1)}, f32[512]{0:T(512)}, u32[]{:S(2)}) copy-start(f32[512]{0:T(512)} %param.35) | copy-start | bytes 6148
  143.4 1.6 copy-start.9
  143.5 1.6 copy-start.14
  146.5 81.1 %all-to-all-start = ((bf16[4,256,512]{2,1,0:T(8,128)(2,1)}), bf16[4,256,512]{2,1,0:T(8,128)(2,1)}, u32[]{:S(2)}, u32[]{:S(2)}) async-start(bf16[4,256,512]{2,1,0:T(8,128)(2,1)} %broadcast_in_dim.19), calls=%async_computation | async-start | bytes 2097152 | tf_op jit(solution)/shard_map/all_to_all | solution.py:40
  292.4 1.0 copy-start.10
  292.4 1.0 copy-start.15
  292.6 1.9 copy-start.1
Sparse Core Ops, SparseCore 0:
  145.1 71.1 all-gather.1
where the time goes:
time: 304 us; the launch traced here: 301 us
  blocking collectives  113 us (37%)
  waiting for transfers between devices  78.7 us (26%)
  matrix products  40.6 us (13%)
  starting transfers between devices  24.1 us (8%)
  local copies, waits for them, and re-layouts  18.5 us (6%)
  between operations  14 us (5%)
  other arithmetic  12.3 us (4%)
    psum x12, blocking collectives, over_axes(): return functools.reduce(lax.psum, axes, x)  88.9 us
    all_gather x1, waiting for transfers between devices, side_by_side(): lax.all_gather(both, axis, axis=dim, tiled=True)  65.4 us
    dot_general x4, matrix products, step_block(): jnp.dot(tile_queries, key_block.T, preferred_element_type=jnp.float32)  17 us
    dot_general x4, matrix products, step_block(): jnp.dot(expo.astype(jnp.bfloat16), value_block, preferred_element_type=jn...  16.3 us
    all_to_all x1, blocking collectives, sent_and_summed(): blocks = lax.all_to_all(in_blocks(x, dim, peers), axis, 0, 0, tiled=True)  16 us
    ppermute x4, waiting for transfers between devices, extended(): after = lax.ppermute(initial, axis, down)  13.2 us
    ppermute x4, starting transfers between devices, extended(): before = lax.ppermute(last, axis, up)  13.1 us
    split x1, local copies, waits for them, and re-layouts, side_by_side(): jnp.split(lax.all_gather(both, axis, axis=dim, tiled=True), ends, axis=al...  11.3 us
  transfers between devices with their start and end apart: 10, of which 5 were waited for; matrix products, arithmetic and copies ran while one was open for 5% of the time, Pallas kernels for 0%

commit v1 on v0

v1 whole, which is shorter than its diff:
```python
import functools

import jax
import jax.numpy as jnp
from jax import lax
from jax.experimental import pallas as pl
from jax.experimental.pallas import tpu as pltpu
from jax.sharding import Mesh
from jax.sharding import PartitionSpec as P

C = 512
GROUPS = 32
AXES = ("tile_0", "tile_1", "tile_2", "head")
TILE = ("tile_0", "tile_1", "tile_2")
MESH = pl.DeviceIdType.MESH
BF = jnp.bfloat16
F32 = jnp.float32
EPS = 1e-06

ROWS, COLS = 2, 128
POS = ROWS * COLS
RING = 4
TILES = 32
SLOTS = 16
CHUNKS = 8
QT = 512
KC = 1024
LPAD = 16
HPAD = 8
NT = (((1,), (1,)), ((), ()))
NN = (((1,), (0,)), ((), ()))


def slot_of(dx, dy):
    if dy == 0:
        return dx
    if dx == 0:
        return 3 + dy
    return 7 + (dx - 1) * 3 + (dy - 1)


def dot(a, b, dims=NN):
    return lax.dot_general(a, b, dims, preferred_element_type=F32)


def copy_to(src, dst, send, recv, dev):
    return pltpu.make_async_remote_copy(
        src_ref=src, dst_ref=dst, send_sem=send, recv_sem=recv, device_id=dev, device_id_type=MESH
    )


def block_kernel(*refs):
    hbm = refs[:18]
    out_hbm = refs[18]
    (
        vecs, w1, w2, wp, ext, tmp, act, acc_c, hext, ar_tx, ar_rx,
        kv, qres, qq, s0, s1, p0, p1, acc0, acc1, m0, m1, l0, l1, a0, a1,
        ctx_tx, lse_tx, ctx_rx, lse_rx, out_v,
        ld, out_sem, h_send, h_recv, ar_send, ar_recv,
        kv_send, kv_recv, d_send, d_recv, q_send, q_recv, c_send, c_recv, e_send, e_recv,
    ) = refs[19:]
    x = lax.axis_index("tile_0")
    y = lax.axis_index("tile_1")
    c = lax.axis_index("tile_2")
    z = lax.axis_index("head")
    t = (x * RING + y) * 2 + c

    def ring(v, i):
        return lax.rem(v + i, RING)

    def tile_dev(dt, dz):
        n = lax.rem(t + dt + TILES, TILES)
        return (n // 8, lax.rem(n // 2, RING), lax.rem(n, 2), lax.rem(z + dz + RING, RING))

    sibling = (x, y, 1 - c, z)

    (lat, g1, b1, cw1, cb1, g2, b2, cw2, cb2, g3, b3, wq, bq, wk, wv, bv, wo, bo) = hbm
    loads = [pltpu.make_async_copy(lat, ext.at[1:3, LPAD : LPAD + COLS], ld.at[0])]
    for i, v in enumerate((g1, b1, cb1, g2, b2, cb2, g3, b3, bq, bv, bo)):
        loads.append(pltpu.make_async_copy(v, vecs.at[i], ld.at[1 + i]))
    loads.append(pltpu.make_async_copy(cw1, w1, ld.at[12]))
    loads.append(pltpu.make_async_copy(cw2, w2, ld.at[13]))
    for i, w in enumerate((wq, wk, wv, wo)):
        loads.append(pltpu.make_async_copy(w, wp.at[i], ld.at[14 + i]))
    for copy in loads:
        copy.start()

    barrier = pltpu.get_barrier_semaphore()
    peers = [sibling]
    for i in range(1, RING):
        peers += [(ring(x, i), y, c, z), (x, ring(y, i), c, z), (x, y, c, ring(z, i))]
    for dt in (-1, 1):
        for dz in (-1, 0, 1):
            peers.append(tile_dev(dt, dz))
    for dev in peers:
        pl.semaphore_signal(barrier, inc=1, device_id=dev, device_id_type=MESH)
    pl.semaphore_wait(barrier, len(peers))

    loads[0].wait()

    def halo(buf, pad, k):
        lo, hi = pad, pad + COLS
        own = slice(lo, hi)
        first, last = slice(lo, lo + pad), slice(hi - pad, hi)
        left, right = slice(0, lo), slice(hi, hi + pad)
        plan = [
            ((1, 2, own), (3, 4, own), (-1, 0)),
            ((2, 3, own), (0, 1, own), (1, 0)),
            ((1, 3, first), (1, 3, right), (0, -1)),
            ((1, 3, last), (1, 3, left), (0, 1)),
            ((1, 2, first), (3, 4, right), (-1, -1)),
            ((1, 2, last), (3, 4, left), (-1, 1)),
            ((2, 3, first), (0, 1, right), (1, -1)),
            ((2, 3, last), (0, 1, left), (1, 1)),
        ]
        copies = []
        for n, (s, d, (dt, dz)) in enumerate(plan):
            copies.append(
                copy_to(
                    buf.at[s[0] : s[1], s[2]], buf.at[d[0] : d[1], d[2]],
                    h_send.at[k, n], h_recv.at[k, n], tile_dev(dt, dz),
                )
            )
        return copies

    def moments(v):
        return jnp.concatenate(
            [jnp.sum(v, axis=0, keepdims=True), jnp.sum(v * v, axis=0, keepdims=True)], axis=0
        )

    STAGES = (("z", 0), ("x", 3), ("y", 6), ("c", 9))

    def stat_copies(k, stage):
        name, base = STAGES[stage]
        copies = []
        for i in range(1, 2 if name == "c" else RING):
            dev = {
                "z": (x, y, c, ring(z, i)),
                "x": (ring(x, i), y, c, z),
                "y": (x, ring(y, i), c, z),
                "c": sibling,
            }[name]
            n = base + i - 1
            copies.append(
                copy_to(ar_tx.at[k, stage], ar_rx.at[k, n], ar_send.at[k, n], ar_recv.at[k, n], dev)
            )
        return copies

    def all_stats(k, local, after=(None, None, None, None)):
        total = local
        pending = []
        for stage in range(4):
            ar_tx[k, stage] = total
            copies = stat_copies(k, stage)
            for copy in copies:
                copy.start()
            if after[stage] is not None:
                after[stage]()
            base = STAGES[stage][1]
            for n, copy in enumerate(copies):
                copy.wait_recv()
                total = total + ar_rx[k, base + n]
            pending += copies
        for copy in pending:
            copy.wait_send()
        return total

    lane = lax.broadcasted_iota(jnp.int32, (8, C), 1)

    def affine(total, gain, shift):
        both = jnp.concatenate([total, jnp.zeros((6, C), F32)], axis=0)
        for d in (1, 2, 4, 8):
            up = pltpu.roll(both, C - d, 1)
            down = pltpu.roll(both, d, 1)
            both = both + jnp.where((lane & d) == 0, up, down)
        members = float(POS * TILES * RING * (C // GROUPS))
        mean = both[0:1] / members
        var = jnp.maximum(both[1:2] / members - mean * mean, 0.0)
        scale = lax.rsqrt(var + EPS) * gain
        return scale, shift - mean * scale

    def activate(buf, pad, width, scale, shift):
        col = lax.broadcasted_iota(jnp.int32, (width, 1), 0)
        edge = ((col >= pad) | (z > 0)) & ((col < pad + COLS) | (z < RING - 1))

        def one_row(r, _):
            inside = ((r > 0) | (t > 0)) & ((r < 3) | (t < TILES - 1))
            u = buf[r].astype(F32) * scale + shift
            u = u / (1.0 + jnp.exp(-u))
            tmp[0:width] = jnp.where(edge & inside, u, 0.0)
            for dj in range(3):
                act[dj, r] = tmp[pad - 1 + dj : pad - 1 + dj + COLS].astype(BF)
            return 0

        lax.fori_loop(0, 4, one_row, 0)

    def conv(weight):
        acc_c[...] = jnp.zeros_like(acc_c)

        def three_taps(di, _):
            part = None
            for dj in range(3):
                a = act[dj, pl.ds(di, 2)].reshape(POS, C)
                d = dot(a, weight[di * 3 + dj])
                part = d if part is None else part + d
            acc_c[...] += part
            return 0

        lax.fori_loop(0, 3, three_taps, 0)

    def vec(i):
        return vecs[i]

    halo0 = halo(ext, LPAD, 0)
    latent = ext[1:3, LPAD : LPAD + COLS].astype(F32).reshape(POS, C)

    def start_halo0():
        for copy in halo0:
            copy.start()

    total = all_stats(0, moments(latent), (start_halo0, None, None, None))
    for copy in loads[1:12]:
        copy.wait()
    for copy in halo0:
        copy.wait_recv()
    scale, shift = affine(total, vec(0), vec(1))
    activate(ext, LPAD, COLS + 2 * LPAD, scale, shift)
    loads[12].wait()
    conv(w1)

    hid = acc_c[...] + vec(2)
    hext[1:3, HPAD : HPAD + COLS] = hid.reshape(ROWS, COLS, C)
    halo1 = halo(hext, HPAD, 1)

    def start_halo1():
        for copy in halo1:
            copy.start()

    total = all_stats(1, moments(hid), (start_halo1, None, None, None))
    for copy in halo1:
        copy.wait_recv()
    scale, shift = affine(total, vec(3), vec(4))
    activate(hext, HPAD, COLS + 2 * HPAD, scale, shift)
    loads[13].wait()
    conv(w2)
    latent = ext[1:3, LPAD : LPAD + COLS].astype(F32).reshape(POS, C)
    res = (latent + (acc_c[...] + vec(5))).astype(BF)
    kv[0, 0] = res

    def half(n, h):
        return kv.at[n, 0, pl.ds(h * COLS, COLS)]

    def own_copy(axis, i, h, n):
        dev = (ring(x, i), y, c, z) if axis == "x" else (x, ring(y, i), c, z)
        back = RING - i
        there = slot_of(back, 0) if axis == "x" else slot_of(0, back)
        return copy_to(half(0, h), half(there, h), kv_send.at[n], kv_recv.at[there, h], dev)

    first_x = [own_copy("x", i, 0, k) for k, i in enumerate((1, 3, 2))]
    first_y = [own_copy("y", i, 1, 3 + k) for k, i in enumerate((1, 3, 2))]
    later_x = [own_copy("x", i, 1, 6 + k) for k, i in enumerate((1, 3, 2))]
    later_y = [own_copy("y", i, 0, 9 + k) for k, i in enumerate((1, 3, 2))]
    onward = []
    for k in range(1, RING):
        for i in (1, 3, 2):
            there = slot_of(k, RING - i)
            here = slot_of(k, 0)
            onward.append(
                copy_to(half(here, 0), half(there, 0), kv_send.at[12 + len(onward)],
                        kv_recv.at[there, 0], (x, ring(y, i), c, z))
            )
            there = slot_of(RING - i, k)
            here = slot_of(0, k)
            onward.append(
                copy_to(half(here, 1), half(there, 1), kv_send.at[12 + len(onward)],
                        kv_recv.at[there, 1], (ring(x, i), y, c, z))
            )
    to_z = [
        copy_to(kv.at[0, 0], qres.at[RING - 1 - i], q_send.at[i - 1], q_recv.at[RING - 1 - i],
                (x, y, c, ring(z, i)))
        for i in (1, 3, 2)
    ]
    pass_own = copy_to(kv.at[0, 0], kv.at[0, 1], d_send.at[0], d_recv.at[0], sibling)

    def begin(copies):
        for copy in copies:
            copy.start()

    res32 = res.astype(F32)
    total = all_stats(
        2,
        moments(res32),
        (
            lambda: begin(to_z + first_x[:2] + first_y),
            lambda: begin(first_x[2:] + later_x),
            lambda: begin(later_y),
            lambda: begin([pass_own]),
        ),
    )
    for k in range(1, RING):
        copy_to(half(0, 0), half(slot_of(k, 0), 0), kv_send.at[0], kv_recv.at[slot_of(k, 0), 0],
                sibling).wait_recv()
        copy_to(half(0, 1), half(slot_of(0, k), 1), kv_send.at[0], kv_recv.at[slot_of(0, k), 1],
                sibling).wait_recv()
    begin(onward)

    scale3, shift3 = affine(total, vec(6), vec(7))
    for copy in loads[14:]:
        copy.wait()
    qres[RING - 1] = res
    for r in range(RING - 1):
        copy_to(kv.at[0, 0], qres.at[r], q_send.at[0], q_recv.at[r], sibling).wait_recv()
    to_exp2 = scale3 * (1.4426950408889634 / C**0.5)
    for r in range(RING):
        normed = (qres[r].astype(F32) * scale3 + shift3).astype(BF)
        q = (dot(normed, wp[0]) + vec(8)).astype(BF)
        qq[r * POS : (r + 1) * POS] = (dot(q, wp[1], NT) * to_exp2).astype(BF)

    for ref in (acc0, acc1, l0, l1):
        ref[...] = jnp.zeros_like(ref)
    for ref in (m0, m1):
        ref[...] = jnp.full_like(ref, -1e30)
    a1[...] = jnp.ones_like(a1)
    p1[...] = jnp.zeros_like(p1)

    def pass_on(n):
        return copy_to(kv.at[n, 0], kv.at[n, 1], d_send.at[n], d_recv.at[n], sibling)

    def wait_half(n, h):
        ref = kv.at[n, 0, pl.ds(h * COLS, COLS)]
        copy_to(ref, ref, kv_send.at[0], kv_recv.at[n, h], sibling).wait_recv()

    def keys(ck):
        return kv[pl.ds(2 * ck, 2)].reshape(KC, C)

    def score(qt, ck, s):
        s[...] = dot(qq[qt * QT : (qt + 1) * QT], keys(ck), NT)

    def soften(s, p, m, l, a):
        step = 32
        for r in range(0, QT, step):
            rows = slice(r, r + step)
            sc = s[rows]
            old = m[rows]
            new = jnp.maximum(old, jnp.max(sc, axis=1, keepdims=True))
            e = jnp.exp2(sc - jnp.concatenate([new] * (KC // 128), axis=1)).astype(BF)
            p[rows] = e
            factor = jnp.exp2(old - new)
            e32 = e.astype(F32)
            part = l[rows] * factor
            for j in range(KC // 128):
                part = part + e32[:, j * 128 : (j + 1) * 128]
            l[rows] = part
            m[rows] = new
            a[rows] = factor

    def weigh(p, acc, a, ck):
        factor = a[...]
        acc[...] = acc[...] * jnp.concatenate([factor] * 4, axis=1) + dot(p[...], keys(ck))

    for k in range(1, 4):
        wait_half(k, 1)
        pass_on(k).start()
    copy_to(kv.at[0, 0], kv.at[0, 1], d_send.at[0], d_recv.at[0], sibling).wait_recv()
    pass_on(1).wait_recv()
    score(0, 0, s0)

    def chunk(ck, _):
        score(1, ck, s1)
        soften(s0, p0, m0, l0, a0)
        weigh(p1, acc1, a1, jnp.maximum(ck - 1, 0))
        nxt = jnp.minimum(ck + 1, CHUNKS - 1)

        @pl.when(ck < CHUNKS - 1)
        def _():
            for j in range(2):
                pass_on(2 * nxt + j).wait_recv()

        ahead = ck + 2

        @pl.when(ahead < CHUNKS)
        def _():
            for j in range(2):
                n = 2 * ahead + j

                @pl.when(n > 6)
                def _():
                    wait_half(n, 0)

                @pl.when(n > 6)
                def _():
                    wait_half(n, 1)

                @pl.when(n <= 6)
                def _():
                    wait_half(n, 0)

                pass_on(n).start()

        score(0, nxt, s0)
        soften(s1, p1, m1, l1, a1)
        weigh(p0, acc0, a0, ck)
        return 0

    lax.fori_loop(0, CHUNKS, chunk, 0)
    weigh(p1, acc1, a1, CHUNKS - 1)

    def finish(r):
        acc, m, l = ((acc0, m0, l0), (acc1, m1, l1))[r // 2]
        rows = slice((r % 2) * POS, (r % 2 + 1) * POS)
        total_l = jnp.sum(l[rows], axis=1, keepdims=True)
        ctx = acc[rows] * (1.0 / total_l) * scale3 + shift3
        return ctx, m[rows] + jnp.log2(total_l)

    sent = []
    for r in range(RING - 1):
        ctx, lse = finish(r)
        ctx_tx[r] = ctx.astype(BF)
        lse_tx[r] = lse.T[0:8]
        there = RING - 2 - r
        dev = (x, y, c, ring(z, r + 1))
        sent.append(copy_to(ctx_tx.at[r], ctx_rx.at[there], c_send.at[r], c_recv.at[there], dev))
        sent.append(copy_to(lse_tx.at[r], lse_rx.at[there], e_send.at[r], e_recv.at[there], dev))
        begin(sent[-2:])
    ctx, lse = finish(RING - 1)
    for copy in sent:
        copy.wait_recv()
    others = [jnp.broadcast_to(lse_rx[r, 0:1], (128, POS)).T for r in range(RING - 1)]
    top = lse
    for o in others:
        top = jnp.maximum(top, o)
    weight = jnp.exp2(lse - top)
    norm = weight
    ctx = ctx * jnp.concatenate([weight] * 4, axis=1)
    for r, o in enumerate(others):
        w = jnp.exp2(o - top)
        norm = norm + w
        ctx = ctx + ctx_rx[r].astype(F32) * jnp.concatenate([w] * 4, axis=1)
    inv = 1.0 / norm
    ctx = (ctx * jnp.concatenate([inv] * 4, axis=1)).astype(BF)
    attended = (dot(ctx, wp[2]) + vec(9)).astype(BF)
    mixed = qres[RING - 1].astype(F32) + dot(attended, wp[3]) + vec(10)
    out_v[...] = mixed.astype(BF).reshape(ROWS, COLS, C)
    done = pltpu.make_async_copy(out_v, out_hbm, out_sem)
    done.start()
    for copy in halo0 + halo1 + first_x + first_y + later_x + later_y + onward + to_z + sent:
        copy.wait_send()
    for n in range(SLOTS):
        pass_on(n).wait_send()
    done.wait()


def per_device(latent, *params):
    row = lambda v: v.reshape(1, C)
    args = [latent]
    for p in params:
        args.append(row(p) if p.ndim == 1 else (p.reshape(9, C, C) if p.ndim == 4 else p))
    dma = pltpu.SemaphoreType.DMA
    v = pltpu.VMEM
    scratch = [
        v((11, 1, C), F32), v((9, C, C), BF), v((9, C, C), BF), v((4, C, C), BF),
        v((4, COLS + 2 * LPAD, C), BF), v((COLS + 2 * LPAD, C), F32), v((3, 4, COLS, C), BF),
        v((POS, C), F32), v((4, COLS + 2 * HPAD, C), F32),
        v((3, 4, 2, C), F32), v((3, 10, 2, C), F32),
        v((SLOTS, 2, POS, C), BF), v((RING, POS, C), BF), v((RING * POS, C), BF),
        v((QT, KC), F32), v((QT, KC), F32), v((QT, KC), BF), v((QT, KC), BF),
        v((QT, C), F32), v((QT, C), F32),
        v((QT, 128), F32), v((QT, 128), F32), v((QT, 128), F32), v((QT, 128), F32),
        v((QT, 128), F32), v((QT, 128), F32),
        v((3, POS, C), BF), v((3, 8, POS), F32), v((3, POS, C), BF), v((3, 8, POS), F32),
        v((ROWS, COLS, C), BF),
        dma((18,)), dma, dma((2, 8)), dma((2, 8)), dma((3, 10)), dma((3, 10)),
        dma((30,)), dma((SLOTS, 2)), dma((SLOTS,)), dma((SLOTS,)), dma((3,)), dma((3,)),
        dma((3,)), dma((3,)), dma((3,)), dma((3,)),
    ]
    return pl.pallas_call(
        block_kernel,
        out_shape=jax.ShapeDtypeStruct((ROWS, COLS, C), BF),
        in_specs=[pl.BlockSpec(memory_space=pl.ANY)] * 18,
        out_specs=pl.BlockSpec(memory_space=pl.ANY),
        scratch_shapes=scratch,
        compiler_params=pltpu.CompilerParams(
            collective_id=0, has_side_effects=True, vmem_limit_bytes=60 * 1024 * 1024
        ),
    )(*args)


def solution(mesh):
    finer = Mesh(mesh.devices.reshape(4, 4, 2, mesh.shape["head"]), AXES)
    return jax.shard_map(
        per_device,
        mesh=finer,
        in_specs=(P(TILE, "head", None),) + (P(),) * 17,
        out_specs=P(TILE, "head", None),
        check_vma=False,
    )
```

time: 304 us -> 104 us (0.34)
  the two profiles are of different devices: /device:TPU:1 before, /device:TPU:6 now
where the time goes in v1:
time: 104 us
  Pallas kernels  102 us (98%)
  local copies, waits for them, and re-layouts  1.67 us (2%)
    pallas_call x1, Pallas kernels, per_device(): pl.pallas_call(block_kernel, out_shape=jax.ShapeDtypeStruct((ROWS, COLS,...  102 us

profile of v1, /device:TPU:6, one launch (start us, length us, event | category | flops | bytes accessed | tf_op | source)
XLA Modules:
  0.0 103.6 jit_solution(2426040157142383393)
XLA Ops:
  0.0 102.0 %shard_map.172 = bf16[2,128,512]{2,1,0:T(8,128)(2,1)} custom-call(bf16[2,128,512]{2,1,0:T(8,128)(2,1)} %refs_0_.1, f32[1,512]{1,0:T(1,128)} %bitcast.15, f32[1,512]{1,0:T(1,128)} %bitcast.16, bf16[9,512,512]{2,1,0:T(8,128)(2,1)} %bitcast.13, f32[1,512]{1,0:T(1,128)} %bitcast.17, f32[1,512]{1,0:T(1,128)} %bitcast.18, f32[1,512]{1,0:T(1,128)} %bitcast.19, ...), custom_call_target="tpu_custom_call" | custom-call | tf_op jit(solution)/shard_map/pallas_call | solution.py:476
  102.0 1.7 %copy.20 = bf16[2,128,512]{2,1,0:T(8,128)(2,1)} copy(bf16[2,128,512]{2,1,0:T(8,128)(2,1)} %shard_map.172) | data formatting | bytes 524288

commit v2 on v1

--- a/solution.py
+++ b/solution.py
@@ -31,12 +31,15 @@
 NN = (((1,), (0,)), ((), ()))
 
 
+FAR = ((1, 1), (3, 3), (1, 3), (3, 1), (2, 1), (1, 2), (3, 2), (2, 3), (2, 2))
+
+
 def slot_of(dx, dy):
     if dy == 0:
         return dx
     if dx == 0:
         return 3 + dy
-    return 7 + (dx - 1) * 3 + (dy - 1)
+    return 7 + FAR.index((dx, dy))
 
 
 def dot(a, b, dims=NN):
@@ -85,10 +88,21 @@
     for copy in loads:
         copy.start()
 
+    for ref in (acc0, acc1, l0, l1):
+        ref[...] = jnp.zeros_like(ref)
+    for ref in (m0, m1):
+        ref[...] = jnp.full_like(ref, -1e30)
+    a1[...] = jnp.ones_like(a1)
+    p1[...] = jnp.zeros_like(p1)
+
     barrier = pltpu.get_barrier_semaphore()
-    peers = [sibling]
-    for i in range(1, RING):
-        peers += [(ring(x, i), y, c, z), (x, ring(y, i), c, z), (x, y, c, ring(z, i))]
+    column = [sibling]
+    for i in (1, 3, 2):
+        column += [(x, y, c, ring(z, i)), (x, y, 1 - c, ring(z, i))]
+    plane = []
+    for i in range(RING):
+        plane += [(ring(x, i), ring(y, j), c, z) for j in range(RING) if i + j > 0]
+    peers = column + plane
     for dt in (-1, 1):
         for dz in (-1, 0, 1):
             peers.append(tile_dev(dt, dz))
@@ -128,35 +142,20 @@
             [jnp.sum(v, axis=0, keepdims=True), jnp.sum(v * v, axis=0, keepdims=True)], axis=0
         )
 
-    STAGES = (("z", 0), ("x", 3), ("y", 6), ("c", 9))
-
-    def stat_copies(k, stage):
-        name, base = STAGES[stage]
-        copies = []
-        for i in range(1, 2 if name == "c" else RING):
-            dev = {
-                "z": (x, y, c, ring(z, i)),
-                "x": (ring(x, i), y, c, z),
-                "y": (x, ring(y, i), c, z),
-                "c": sibling,
-            }[name]
-            n = base + i - 1
-            copies.append(
-                copy_to(ar_tx.at[k, stage], ar_rx.at[k, n], ar_send.at[k, n], ar_recv.at[k, n], dev)
-            )
-        return copies
-
-    def all_stats(k, local, after=(None, None, None, None)):
+    def all_stats(k, local, after_first, after_second):
         total = local
         pending = []
-        for stage in range(4):
+        for stage, devices, after in ((0, column, after_first), (1, plane, after_second)):
+            base = stage * len(column)
             ar_tx[k, stage] = total
-            copies = stat_copies(k, stage)
+            copies = [
+                copy_to(ar_tx.at[k, stage], ar_rx.at[k, base + n], ar_send.at[k, base + n],
+                        ar_recv.at[k, base + n], dev)
+                for n, dev in enumerate(devices)
+            ]
             for copy in copies:
                 copy.start()
-            if after[stage] is not None:
-                after[stage]()
-            base = STAGES[stage][1]
+            after()
             for n, copy in enumerate(copies):
                 copy.wait_recv()
                 total = total + ar_rx[k, base + n]
@@ -218,7 +217,7 @@
         for copy in halo0:
             copy.start()
 
-    total = all_stats(0, moments(latent), (start_halo0, None, None, None))
+    total = all_stats(0, moments(latent), start_halo0, lambda: None)
     for copy in loads[1:12]:
         copy.wait()
     for copy in halo0:
@@ -236,7 +235,7 @@
         for copy in halo1:
             copy.start()
 
-    total = all_stats(1, moments(hid), (start_halo1, None, None, None))
+    total = all_stats(1, moments(hid), start_halo1, lambda: None)
     for copy in halo1:
         copy.wait_recv()
     scale, shift = affine(total, vec(3), vec(4))
@@ -261,20 +260,16 @@
     later_x = [own_copy("x", i, 1, 6 + k) for k, i in enumerate((1, 3, 2))]
     later_y = [own_copy("y", i, 0, 9 + k) for k, i in enumerate((1, 3, 2))]
     onward = []
-    for k in range(1, RING):
-        for i in (1, 3, 2):
-            there = slot_of(k, RING - i)
-            here = slot_of(k, 0)
-            onward.append(
-                copy_to(half(here, 0), half(there, 0), kv_send.at[12 + len(onward)],
-                        kv_recv.at[there, 0], (x, ring(y, i), c, z))
-            )
-            there = slot_of(RING - i, k)
-            here = slot_of(0, k)
-            onward.append(
-                copy_to(half(here, 1), half(there, 1), kv_send.at[12 + len(onward)],
-                        kv_recv.at[there, 1], (ring(x, i), y, c, z))
-            )
+    for dx, dy in FAR:
+        there = slot_of(dx, dy)
+        onward.append(
+            copy_to(half(slot_of(dx, 0), 0), half(there, 0), kv_send.at[12 + len(onward)],
+                    kv_recv.at[there, 0], (x, ring(y, RING - dy), c, z))
+        )
+        onward.append(
+            copy_to(half(slot_of(0, dy), 1), half(there, 1), kv_send.at[12 + len(onward)],
+                    kv_recv.at[there, 1], (ring(x, RING - dx), y, c, z))
+        )
     to_z = [
         copy_to(kv.at[0, 0], qres.at[RING - 1 - i], q_send.at[i - 1], q_recv.at[RING - 1 - i],
                 (x, y, c, ring(z, i)))
@@ -290,12 +285,8 @@
     total = all_stats(
         2,
         moments(res32),
-        (
-            lambda: begin(to_z + first_x[:2] + first_y),
-            lambda: begin(first_x[2:] + later_x),
-            lambda: begin(later_y),
-            lambda: begin([pass_own]),
-        ),
+        lambda: begin(to_z + first_x[:2] + first_y[:2] + [pass_own]),
+        lambda: begin(first_x[2:] + first_y[2:] + later_x + later_y),
     )
     for k in range(1, RING):
         copy_to(half(0, 0), half(slot_of(k, 0), 0), kv_send.at[0], kv_recv.at[slot_of(k, 0), 0],
@@ -308,20 +299,14 @@
     for copy in loads[14:]:
         copy.wait()
     qres[RING - 1] = res
-    for r in range(RING - 1):
-        copy_to(kv.at[0, 0], qres.at[r], q_send.at[0], q_recv.at[r], sibling).wait_recv()
     to_exp2 = scale3 * (1.4426950408889634 / C**0.5)
-    for r in range(RING):
-        normed = (qres[r].astype(F32) * scale3 + shift3).astype(BF)
+    for tile in (1, 0):
+        for r in range(2 * tile, min(2 * tile + 2, RING - 1)):
+            copy_to(kv.at[0, 0], qres.at[r], q_send.at[0], q_recv.at[r], sibling).wait_recv()
+        both = qres[2 * tile : 2 * tile + 2].reshape(QT, C)
+        normed = (both.astype(F32) * scale3 + shift3).astype(BF)
         q = (dot(normed, wp[0]) + vec(8)).astype(BF)
-        qq[r * POS : (r + 1) * POS] = (dot(q, wp[1], NT) * to_exp2).astype(BF)
-
-    for ref in (acc0, acc1, l0, l1):
-        ref[...] = jnp.zeros_like(ref)
-    for ref in (m0, m1):
-        ref[...] = jnp.full_like(ref, -1e30)
-    a1[...] = jnp.ones_like(a1)
-    p1[...] = jnp.zeros_like(p1)
+        qq[tile * QT : (tile + 1) * QT] = (dot(q, wp[1], NT) * to_exp2).astype(BF)
 
     def pass_on(n):
         return copy_to(kv.at[n, 0], kv.at[n, 1], d_send.at[n], d_recv.at[n], sibling)
@@ -358,62 +343,73 @@
         factor = a[...]
         acc[...] = acc[...] * jnp.concatenate([factor] * 4, axis=1) + dot(p[...], keys(ck))
 
-    for k in range(1, 4):
-        wait_half(k, 1)
-        pass_on(k).start()
-    copy_to(kv.at[0, 0], kv.at[0, 1], d_send.at[0], d_recv.at[0], sibling).wait_recv()
+    acc, m, l = (acc0, acc1), (m0, m1), (l0, l1)
+    s, p, a = (s0, s1), (p0, p1), (a0, a1)
+
+    def arrived(n):
+        if isinstance(n, int):
+            if n < 4 or n > 6:
+                wait_half(n, 1)
+            if n > 3:
+                wait_half(n, 0)
+        pass_on(n).start()
+
+    def ready(ck):
+        for j in range(2):
+            pass_on(2 * ck + j).wait_recv()
+
+    def step(b, score_of, soft_of, weigh_of):
+        if weigh_of is not None:
+            tile, ck = weigh_of
+            weigh(p[1 - b], acc[tile], a[1 - b], ck)
+        if score_of is not None:
+            score(*score_of, s[1 - b])
+        if soft_of is not None:
+            soften(s[b], p[b], m[soft_of], l[soft_of], a[b])
+
+    for n in range(1, 4):
+        arrived(n)
+    pass_on(0).wait_recv()
     pass_on(1).wait_recv()
     score(0, 0, s0)
 
     def chunk(ck, _):
-        score(1, ck, s1)
-        soften(s0, p0, m0, l0, a0)
-        weigh(p1, acc1, a1, jnp.maximum(ck - 1, 0))
-        nxt = jnp.minimum(ck + 1, CHUNKS - 1)
-
-        @pl.when(ck < CHUNKS - 1)
-        def _():
-            for j in range(2):
-                pass_on(2 * nxt + j).wait_recv()
-
-        ahead = ck + 2
-
-        @pl.when(ahead < CHUNKS)
-        def _():
-            for j in range(2):
-                n = 2 * ahead + j
-
-                @pl.when(n > 6)
-                def _():
-                    wait_half(n, 0)
-
-                @pl.when(n > 6)
-                def _():
-                    wait_half(n, 1)
-
-                @pl.when(n <= 6)
-                def _():
-                    wait_half(n, 0)
-
-                pass_on(n).start()
-
-        score(0, nxt, s0)
-        soften(s1, p1, m1, l1, a1)
-        weigh(p0, acc0, a0, ck)
+        first = 2 * ck + 4
+        for n in (first, first + 1):
+            wait_half(n, 0)
+
+            @pl.when(n > 6)
+            def _():
+                wait_half(n, 1)
+
+            pass_on(n).start()
+        ready(ck + 1)
+        step(0, (1, ck), 0, (1, jnp.maximum(ck - 1, 0)))
+        step(1, (0, ck + 1), 1, (0, ck))
         return 0
 
-    lax.fori_loop(0, CHUNKS, chunk, 0)
-    weigh(p1, acc1, a1, CHUNKS - 1)
-
+    lax.fori_loop(0, 4, chunk, 0)
+    arrived(12)
+    arrived(13)
+    ready(5)
+    step(0, (0, 5), 0, (1, 3))
+    arrived(14)
+    arrived(15)
+    ready(6)
+    step(1, (0, 6), 0, (0, 4))
+    ready(7)
+    step(0, (0, 7), 0, (0, 5))
+    step(1, (1, 4), 0, (0, 6))
+    step(0, (1, 5), 1, (0, 7))
     def finish(r):
-        acc, m, l = ((acc0, m0, l0), (acc1, m1, l1))[r // 2]
         rows = slice((r % 2) * POS, (r % 2 + 1) * POS)
-        total_l = jnp.sum(l[rows], axis=1, keepdims=True)
-        ctx = acc[rows] * (1.0 / total_l) * scale3 + shift3
-        return ctx, m[rows] + jnp.log2(total_l)
+        total_l = jnp.sum(l[r // 2][rows], axis=1, keepdims=True)
+        ctx = acc[r // 2][rows] * (1.0 / total_l) * scale3 + shift3
+        return ctx, m[r // 2][rows] + jnp.log2(total_l)
 
     sent = []
-    for r in range(RING - 1):
+
+    def send(r):
         ctx, lse = finish(r)
         ctx_tx[r] = ctx.astype(BF)
         lse_tx[r] = lse.T[0:8]
@@ -422,6 +418,14 @@
         sent.append(copy_to(ctx_tx.at[r], ctx_rx.at[there], c_send.at[r], c_recv.at[there], dev))
         sent.append(copy_to(lse_tx.at[r], lse_rx.at[there], e_send.at[r], e_recv.at[there], dev))
         begin(sent[-2:])
+
+    send(1)
+    send(0)
+    step(1, (1, 6), 1, (1, 4))
+    step(0, (1, 7), 1, (1, 5))
+    step(1, None, 1, (1, 6))
+    step(0, None, None, (1, 7))
+    send(2)
     ctx, lse = finish(RING - 1)
     for copy in sent:
         copy.wait_recv()
@@ -461,7 +465,7 @@
         v((11, 1, C), F32), v((9, C, C), BF), v((9, C, C), BF), v((4, C, C), BF),
         v((4, COLS + 2 * LPAD, C), BF), v((COLS + 2 * LPAD, C), F32), v((3, 4, COLS, C), BF),
         v((POS, C), F32), v((4, COLS + 2 * HPAD, C), F32),
-        v((3, 4, 2, C), F32), v((3, 10, 2, C), F32),
+        v((3, 2, 2, C), F32), v((3, 22, 2, C), F32),
         v((SLOTS, 2, POS, C), BF), v((RING, POS, C), BF), v((RING * POS, C), BF),
         v((QT, KC), F32), v((QT, KC), F32), v((QT, KC), BF), v((QT, KC), BF),
         v((QT, C), F32), v((QT, C), F32),
@@ -469,7 +473,7 @@
         v((QT, 128), F32), v((QT, 128), F32),
         v((3, POS, C), BF), v((3, 8, POS), F32), v((3, POS, C), BF), v((3, 8, POS), F32),
         v((ROWS, COLS, C), BF),
-        dma((18,)), dma, dma((2, 8)), dma((2, 8)), dma((3, 10)), dma((3, 10)),
+        dma((18,)), dma, dma((2, 8)), dma((2, 8)), dma((3, 22)), dma((3, 22)),
         dma((30,)), dma((SLOTS, 2)), dma((SLOTS,)), dma((SLOTS,)), dma((3,)), dma((3,)),
         dma((3,)), dma((3,)), dma((3,)), dma((3,)),
     ]

time: 104 us -> 89.9 us (0.86)
  the two profiles are of different devices: /device:TPU:6 before, /device:TPU:1 now
where the time goes in v2:
time: 89.9 us; the launch traced here: 89.8 us
  Pallas kernels  88.1 us (98%)
  local copies, waits for them, and re-layouts  1.67 us (2%)
    pallas_call x1, Pallas kernels, per_device(): pl.pallas_call(block_kernel, out_shape=jax.ShapeDtypeStruct((ROWS, COLS,...  88.1 us

profile of v2, /device:TPU:1, one launch (start us, length us, event | category | flops | bytes accessed | tf_op | source)
XLA Modules:
  0.0 89.8 jit_solution(17416027734099273728)
XLA Ops:
  0.0 88.1 %shard_map.172 = bf16[2,128,512]{2,1,0:T(8,128)(2,1)} custom-call(bf16[2,128,512]{2,1,0:T(8,128)(2,1)} %refs_0_.1, f32[1,512]{1,0:T(1,128)} %bitcast.15, f32[1,512]{1,0:T(1,128)} %bitcast.16, bf16[9,512,512]{2,1,0:T(8,128)(2,1)} %bitcast.13, f32[1,512]{1,0:T(1,128)} %bitcast.17, f32[1,512]{1,0:T(1,128)} %bitcast.18, f32[1,512]{1,0:T(1,128)} %bitcast.19, ...), custom_call_target="tpu_custom_call" | custom-call | tf_op jit(solution)/shard_map/pallas_call | solution.py:480
  88.1 1.7 %copy.20 = bf16[2,128,512]{2,1,0:T(8,128)(2,1)} copy(bf16[2,128,512]{2,1,0:T(8,128)(2,1)} %shard_map.172) | data formatting | bytes 524288

commit v3 on v2

--- a/solution.py
+++ b/solution.py
@@ -31,15 +31,14 @@
 NN = (((1,), (0,)), ((), ()))
 
 
-FAR = ((1, 1), (3, 3), (1, 3), (3, 1), (2, 1), (1, 2), (3, 2), (2, 3), (2, 2))
+ORDER = (
+    (0, 0), (1, 0), (3, 0), (0, 1), (0, 3), (1, 1), (3, 3), (2, 0),
+    (0, 2), (1, 3), (3, 1), (2, 1), (1, 2), (3, 2), (2, 3), (2, 2),
+)
 
 
 def slot_of(dx, dy):
-    if dy == 0:
-        return dx
-    if dx == 0:
-        return 3 + dy
-    return 7 + FAR.index((dx, dy))
+    return ORDER.index((dx, dy))
 
 
 def dot(a, b, dims=NN):
@@ -54,12 +53,12 @@
 
 def block_kernel(*refs):
     hbm = refs[:18]
-    out_hbm = refs[18]
+    out = refs[18]
     (
         vecs, w1, w2, wp, ext, tmp, act, acc_c, hext, ar_tx, ar_rx,
         kv, qres, qq, s0, s1, p0, p1, acc0, acc1, m0, m1, l0, l1, a0, a1,
-        ctx_tx, lse_tx, ctx_rx, lse_rx, out_v,
-        ld, out_sem, h_send, h_recv, ar_send, ar_recv,
+        ctx_tx, lse_tx, ctx_rx, lse_rx,
+        ld, h_send, h_recv, ar_send, ar_recv,
         kv_send, kv_recv, d_send, d_recv, q_send, q_recv, c_send, c_recv, e_send, e_recv,
     ) = refs[19:]
     x = lax.axis_index("tile_0")
@@ -257,19 +256,32 @@
 
     first_x = [own_copy("x", i, 0, k) for k, i in enumerate((1, 3, 2))]
     first_y = [own_copy("y", i, 1, 3 + k) for k, i in enumerate((1, 3, 2))]
-    later_x = [own_copy("x", i, 1, 6 + k) for k, i in enumerate((1, 3, 2))]
-    later_y = [own_copy("y", i, 0, 9 + k) for k, i in enumerate((1, 3, 2))]
+    later_x = [own_copy("x", i, 1, 6 + k) for k, i in enumerate((1, 3))]
+    later_y = [own_copy("y", i, 0, 8 + k) for k, i in enumerate((1, 3))]
+    moved = []
+
+    def hand_on(axis, h, source, there):
+        step = (source[0] - there[0], source[1] - there[1])
+        dev = (ring(x, step[0] % RING), y, c, z) if axis == "x" else (x, ring(y, step[1] % RING), c, z)
+        n = slot_of(*there)
+        copy = copy_to(half(slot_of(*source), h), half(n, h), kv_send.at[10 + len(moved)],
+                       kv_recv.at[n, h], dev)
+        moved.append(copy)
+        return copy
+
     onward = []
-    for dx, dy in FAR:
-        there = slot_of(dx, dy)
-        onward.append(
-            copy_to(half(slot_of(dx, 0), 0), half(there, 0), kv_send.at[12 + len(onward)],
-                    kv_recv.at[there, 0], (x, ring(y, RING - dy), c, z))
-        )
-        onward.append(
-            copy_to(half(slot_of(0, dy), 1), half(there, 1), kv_send.at[12 + len(onward)],
-                    kv_recv.at[there, 1], (ring(x, RING - dx), y, c, z))
-        )
+    for dx, dy in ORDER:
+        if dx and dy:
+            if dy != 2 or dx == 2:
+                onward.append(hand_on("y", 0, (dx, 0), (dx, dy)))
+            if dx != 2 or dy == 2:
+                onward.append(hand_on("x", 1, (0, dy), (dx, dy)))
+    relays = {
+        (1, 0): [hand_on("x", 1, (1, 0), (2, 0))],
+        (0, 1): [hand_on("y", 0, (0, 1), (0, 2))],
+        (1, 1): [hand_on("y", 0, (1, 1), (1, 2)), hand_on("x", 1, (1, 1), (2, 1))],
+        (3, 3): [hand_on("y", 0, (3, 3), (3, 2)), hand_on("x", 1, (3, 3), (2, 3))],
+    }
     to_z = [
         copy_to(kv.at[0, 0], qres.at[RING - 1 - i], q_send.at[i - 1], q_recv.at[RING - 1 - i],
                 (x, y, c, ring(z, i)))
@@ -295,6 +307,26 @@
                 sibling).wait_recv()
     begin(onward)
 
+    def pass_on(n):
+        return copy_to(kv.at[n, 0], kv.at[n, 1], d_send.at[n], d_recv.at[n], sibling)
+
+    def wait_half(n, h):
+        ref = kv.at[n, 0, pl.ds(h * COLS, COLS)]
+        copy_to(ref, ref, kv_send.at[0], kv_recv.at[n, h], sibling).wait_recv()
+
+    def arrived(n):
+        dx, dy = ORDER[n]
+        if dx:
+            wait_half(n, 1)
+        if dy:
+            wait_half(n, 0)
+        begin(relays.get((dx, dy), []))
+        pass_on(n).start()
+
+    def ready(ck):
+        for j in range(2):
+            pass_on(2 * ck + j).wait_recv()
+
     scale3, shift3 = affine(total, vec(6), vec(7))
     for copy in loads[14:]:
         copy.wait()
@@ -307,13 +339,10 @@
         normed = (both.astype(F32) * scale3 + shift3).astype(BF)
         q = (dot(normed, wp[0]) + vec(8)).astype(BF)
         qq[tile * QT : (tile + 1) * QT] = (dot(q, wp[1], NT) * to_exp2).astype(BF)
-
-    def pass_on(n):
-        return copy_to(kv.at[n, 0], kv.at[n, 1], d_send.at[n], d_recv.at[n], sibling)
-
-    def wait_half(n, h):
-        ref = kv.at[n, 0, pl.ds(h * COLS, COLS)]
-        copy_to(ref, ref, kv_send.at[0], kv_recv.at[n, h], sibling).wait_recv()
+        if tile == 1:
+            arrived(1)
+            arrived(2)
+            arrived(3)
 
     def keys(ck):
         return kv[pl.ds(2 * ck, 2)].reshape(KC, C)
@@ -343,20 +372,39 @@
         factor = a[...]
         acc[...] = acc[...] * jnp.concatenate([factor] * 4, axis=1) + dot(p[...], keys(ck))
 
+    def score_two(r, ck, s):
+        for j in range(2):
+            s[j * POS : (j + 1) * POS] = dot(qq[r * POS : (r + 1) * POS], keys(ck + j), NT)
+
+    def soften_two(r, s, p, m, l, a):
+        step, base = 16, (r % 2) * POS
+        for i in range(0, POS, step):
+            rows, at = slice(base + i, base + i + step), slice(i, i + step)
+            low = slice(POS + i, POS + i + step)
+            sc = jnp.concatenate([s[at], s[low]], axis=1)
+            old = m[rows]
+            new = jnp.maximum(old, jnp.max(sc, axis=1, keepdims=True))
+            e = jnp.exp2(sc - jnp.concatenate([new] * (2 * KC // 128), axis=1)).astype(BF)
+            p[at] = e[:, :KC]
+            p[low] = e[:, KC:]
+            factor = jnp.exp2(old - new)
+            e32 = e.astype(F32)
+            part = l[rows] * factor
+            for j in range(2 * KC // 128):
+                part = part + e32[:, j * 128 : (j + 1) * 128]
+            l[rows] = part
+            m[rows] = new
+            a[at] = factor
+
+    def weigh_two(r, p, acc, a, ck):
+        rows = slice((r % 2) * POS, (r % 2 + 1) * POS)
+        factor = jnp.concatenate([a[0:POS]] * 4, axis=1)
+        acc[rows] = acc[rows] * factor + (
+            dot(p[0:POS], keys(ck)) + dot(p[POS : 2 * POS], keys(ck + 1))
+        )
+
     acc, m, l = (acc0, acc1), (m0, m1), (l0, l1)
     s, p, a = (s0, s1), (p0, p1), (a0, a1)
-
-    def arrived(n):
-        if isinstance(n, int):
-            if n < 4 or n > 6:
-                wait_half(n, 1)
-            if n > 3:
-                wait_half(n, 0)
-        pass_on(n).start()
-
-    def ready(ck):
-        for j in range(2):
-            pass_on(2 * ck + j).wait_recv()
 
     def step(b, score_of, soft_of, weigh_of):
         if weigh_of is not None:
@@ -367,40 +415,36 @@
         if soft_of is not None:
             soften(s[b], p[b], m[soft_of], l[soft_of], a[b])
 
-    for n in range(1, 4):
-        arrived(n)
-    pass_on(0).wait_recv()
-    pass_on(1).wait_recv()
+    arrived(4)
+    ready(0)
     score(0, 0, s0)
-
-    def chunk(ck, _):
-        first = 2 * ck + 4
-        for n in (first, first + 1):
-            wait_half(n, 0)
-
-            @pl.when(n > 6)
-            def _():
-                wait_half(n, 1)
-
-            pass_on(n).start()
-        ready(ck + 1)
-        step(0, (1, ck), 0, (1, jnp.maximum(ck - 1, 0)))
-        step(1, (0, ck + 1), 1, (0, ck))
-        return 0
-
-    lax.fori_loop(0, 4, chunk, 0)
+    step(0, (1, 0), 0, None)
+    arrived(5)
+    arrived(6)
+    ready(1)
+    step(1, (0, 1), 1, (0, 0))
+    arrived(7)
+    arrived(8)
+    ready(2)
+    step(0, (1, 1), 0, (1, 0))
+    step(1, (0, 2), 1, (0, 1))
+    arrived(9)
+    arrived(10)
+    ready(3)
+    step(0, (1, 2), 0, (1, 1))
+    step(1, (0, 3), 1, (0, 2))
+    arrived(11)
     arrived(12)
+    step(0, (1, 3), 0, (1, 2))
     arrived(13)
-    ready(5)
-    step(0, (0, 5), 0, (1, 3))
     arrived(14)
     arrived(15)
+    ready(4)
+    ready(5)
+    step(1, None, 1, (0, 3))
+    score_two(1, 4, s0)
     ready(6)
-    step(1, (0, 6), 0, (0, 4))
     ready(7)
-    step(0, (0, 7), 0, (0, 5))
-    step(1, (1, 4), 0, (0, 6))
-    step(0, (1, 5), 1, (0, 7))
     def finish(r):
         rows = slice((r % 2) * POS, (r % 2 + 1) * POS)
         total_l = jnp.sum(l[r // 2][rows], axis=1, keepdims=True)
@@ -419,13 +463,20 @@
         sent.append(copy_to(lse_tx.at[r], lse_rx.at[there], e_send.at[r], e_recv.at[there], dev))
         begin(sent[-2:])
 
-    send(1)
-    send(0)
-    step(1, (1, 6), 1, (1, 4))
-    step(0, (1, 7), 1, (1, 5))
-    step(1, None, 1, (1, 6))
-    step(0, None, None, (1, 7))
-    send(2)
+    units = [(r, ck) for r in (1, 0, 2, 3) for ck in (4, 6)]
+    for u, (r, ck) in enumerate(units):
+        b = u % 2
+        if u == 0:
+            weigh(p1, acc1, a1, 3)
+        else:
+            last, at = units[u - 1]
+            weigh_two(last, p[1 - b], acc[last // 2], a[1 - b], at)
+        if u + 1 < len(units):
+            score_two(*units[u + 1], s[1 - b])
+        soften_two(r, s[b], p[b], m[r // 2], l[r // 2], a[b])
+        if u in (2, 4, 6):
+            send(units[u - 1][0])
+    weigh_two(RING - 1, p1, acc1, a1, 6)
     ctx, lse = finish(RING - 1)
     for copy in sent:
         copy.wait_recv()
@@ -444,14 +495,11 @@
     ctx = (ctx * jnp.concatenate([inv] * 4, axis=1)).astype(BF)
     attended = (dot(ctx, wp[2]) + vec(9)).astype(BF)
     mixed = qres[RING - 1].astype(F32) + dot(attended, wp[3]) + vec(10)
-    out_v[...] = mixed.astype(BF).reshape(ROWS, COLS, C)
-    done = pltpu.make_async_copy(out_v, out_hbm, out_sem)
-    done.start()
-    for copy in halo0 + halo1 + first_x + first_y + later_x + later_y + onward + to_z + sent:
+    out[...] = mixed.astype(BF).reshape(ROWS, COLS, C)
+    for copy in halo0 + halo1 + first_x + first_y + later_x + later_y + moved + to_z + sent:
         copy.wait_send()
     for n in range(SLOTS):
         pass_on(n).wait_send()
-    done.wait()
 
 
 def per_device(latent, *params):
@@ -472,8 +520,7 @@
         v((QT, 128), F32), v((QT, 128), F32), v((QT, 128), F32), v((QT, 128), F32),
         v((QT, 128), F32), v((QT, 128), F32),
         v((3, POS, C), BF), v((3, 8, POS), F32), v((3, POS, C), BF), v((3, 8, POS), F32),
-        v((ROWS, COLS, C), BF),
-        dma((18,)), dma, dma((2, 8)), dma((2, 8)), dma((3, 22)), dma((3, 22)),
+        dma((18,)), dma((2, 8)), dma((2, 8)), dma((3, 22)), dma((3, 22)),
         dma((30,)), dma((SLOTS, 2)), dma((SLOTS,)), dma((SLOTS,)), dma((3,)), dma((3,)),
         dma((3,)), dma((3,)), dma((3,)), dma((3,)),
     ]
@@ -481,7 +528,7 @@
         block_kernel,
         out_shape=jax.ShapeDtypeStruct((ROWS, COLS, C), BF),
         in_specs=[pl.BlockSpec(memory_space=pl.ANY)] * 18,
-        out_specs=pl.BlockSpec(memory_space=pl.ANY),
+        out_specs=pl.BlockSpec(memory_space=pltpu.VMEM),
         scratch_shapes=scratch,
         compiler_params=pltpu.CompilerParams(
             collective_id=0, has_side_effects=True, vmem_limit_bytes=60 * 1024 * 1024

time: 89.9 us -> 92.6 us (1.030)
  Pallas kernels: 88.1 us -> 90.8 us
    pallas_call x1, Pallas kernels: 88.1 us -> 90.8 us  [per_device(): pl.pallas_call(block_kernel, out_shape=jax.ShapeDtypeStruct((ROWS, COLS,...]
where the time goes in v3:
time: 92.6 us; the launch traced here: 92.5 us
  Pallas kernels  90.8 us (98%)
  local copies, waits for them, and re-layouts  1.67 us (2%)
    pallas_call x1, Pallas kernels, per_device(): pl.pallas_call(block_kernel, out_shape=jax.ShapeDtypeStruct((ROWS, COLS,...  90.8 us

profile of v3, /device:TPU:1, one launch (start us, length us, event | category | flops | bytes accessed | tf_op | source)
XLA Modules:
  0.0 92.5 jit_solution(4695635986658265237)
XLA Ops:
  0.0 90.8 %shard_map.172 = bf16[2,128,512]{2,1,0:T(8,128)(2,1)} custom-call(bf16[2,128,512]{2,1,0:T(8,128)(2,1)} %refs_0_.1, f32[1,512]{1,0:T(1,128)} %bitcast.15, f32[1,512]{1,0:T(1,128)} %bitcast.16, bf16[9,512,512]{2,1,0:T(8,128)(2,1)} %bitcast.13, f32[1,512]{1,0:T(1,128)} %bitcast.17, f32[1,512]{1,0:T(1,128)} %bitcast.18, f32[1,512]{1,0:T(1,128)} %bitcast.19, ...), custom_call_target="tpu_custom_call" | custom-call | tf_op jit(solution)/shard_map/pallas_call | solution.py:527
  90.8 1.7 %copy.20 = bf16[2,128,512]{2,1,0:T(8,128)(2,1)} copy(bf16[2,128,512]{2,1,0:T(8,128)(2,1)} %shard_map.172) | data formatting | bytes 524288

commit v4 on v3

--- a/solution.py
+++ b/solution.py
@@ -32,9 +32,10 @@
 
 
 ORDER = (
-    (0, 0), (1, 0), (3, 0), (0, 1), (0, 3), (1, 1), (3, 3), (2, 0),
-    (0, 2), (1, 3), (3, 1), (2, 1), (1, 2), (3, 2), (2, 3), (2, 2),
+    (0, 0), (1, 0), (3, 0), (0, 1), (0, 3), (1, 1), (3, 3), (1, 3),
+    (3, 1), (2, 0), (0, 2), (2, 2), (1, 2), (2, 1), (3, 2), (2, 3),
 )
+OWNER = (1, 3, 2, 0)
 
 
 def slot_of(dx, dy):
@@ -141,11 +142,13 @@
             [jnp.sum(v, axis=0, keepdims=True), jnp.sum(v * v, axis=0, keepdims=True)], axis=0
         )
 
-    def all_stats(k, local, after_first, after_second):
+    def all_stats(k, local, after_first, after_second, plane_first=False):
         total = local
         pending = []
-        for stage, devices, after in ((0, column, after_first), (1, plane, after_second)):
-            base = stage * len(column)
+        stages = [(0, column), (len(column), plane)]
+        if plane_first:
+            stages.reverse()
+        for stage, ((base, devices), after) in enumerate(zip(stages, (after_first, after_second))):
             ar_tx[k, stage] = total
             copies = [
                 copy_to(ar_tx.at[k, stage], ar_rx.at[k, base + n], ar_send.at[k, base + n],
@@ -269,44 +272,50 @@
         moved.append(copy)
         return copy
 
-    onward = []
-    for dx, dy in ORDER:
-        if dx and dy:
-            if dy != 2 or dx == 2:
-                onward.append(hand_on("y", 0, (dx, 0), (dx, dy)))
-            if dx != 2 or dy == 2:
-                onward.append(hand_on("x", 1, (0, dy), (dx, dy)))
+    onward = [
+        copy
+        for far in ((1, 1), (3, 3), (1, 3), (3, 1))
+        for copy in (hand_on("y", 0, (far[0], 0), far), hand_on("x", 1, (0, far[1]), far))
+    ]
+    onward_two = [hand_on("y", 0, (2, 0), (2, 2)), hand_on("x", 1, (0, 2), (2, 2))]
+    for k in (1, 3):
+        onward_two.append(hand_on("y", 0, (2, 0), (2, k)))
+        onward_two.append(hand_on("x", 1, (0, 2), (k, 2)))
     relays = {
         (1, 0): [hand_on("x", 1, (1, 0), (2, 0))],
         (0, 1): [hand_on("y", 0, (0, 1), (0, 2))],
         (1, 1): [hand_on("y", 0, (1, 1), (1, 2)), hand_on("x", 1, (1, 1), (2, 1))],
         (3, 3): [hand_on("y", 0, (3, 3), (3, 2)), hand_on("x", 1, (3, 3), (2, 3))],
     }
-    to_z = [
-        copy_to(kv.at[0, 0], qres.at[RING - 1 - i], q_send.at[i - 1], q_recv.at[RING - 1 - i],
-                (x, y, c, ring(z, i)))
-        for i in (1, 3, 2)
-    ]
+    to_z = []
+    for i in (1, 3, 2):
+        place = OWNER.index(RING - i)
+        to_z.append(copy_to(kv.at[0, 0], qres.at[place], q_send.at[i - 1], q_recv.at[place],
+                            (x, y, c, ring(z, i))))
     pass_own = copy_to(kv.at[0, 0], kv.at[0, 1], d_send.at[0], d_recv.at[0], sibling)
 
     def begin(copies):
         for copy in copies:
             copy.start()
+
+    def far_half(n, h):
+        return copy_to(half(0, h), half(n, h), kv_send.at[0], kv_recv.at[n, h], sibling)
+
+    def forward():
+        begin([pass_own] + to_z[2:])
+        for k in (1, 3):
+            far_half(slot_of(k, 0), 0).wait_recv()
+            far_half(slot_of(0, k), 1).wait_recv()
+        begin(onward)
 
     res32 = res.astype(F32)
     total = all_stats(
         2,
         moments(res32),
-        lambda: begin(to_z + first_x[:2] + first_y[:2] + [pass_own]),
-        lambda: begin(first_x[2:] + first_y[2:] + later_x + later_y),
+        lambda: begin(first_x + first_y + later_x + later_y + to_z[:2]),
+        forward,
+        plane_first=True,
     )
-    for k in range(1, RING):
-        copy_to(half(0, 0), half(slot_of(k, 0), 0), kv_send.at[0], kv_recv.at[slot_of(k, 0), 0],
-                sibling).wait_recv()
-        copy_to(half(0, 1), half(slot_of(0, k), 1), kv_send.at[0], kv_recv.at[slot_of(0, k), 1],
-                sibling).wait_recv()
-    begin(onward)
-
     def pass_on(n):
         return copy_to(kv.at[n, 0], kv.at[n, 1], d_send.at[n], d_recv.at[n], sibling)
 
@@ -327,22 +336,27 @@
         for j in range(2):
             pass_on(2 * ck + j).wait_recv()
 
+    for n in range(1, 5):
+        arrived(n)
+    far_half(slot_of(2, 0), 0).wait_recv()
+    far_half(slot_of(0, 2), 1).wait_recv()
+    begin(onward_two)
+
     scale3, shift3 = affine(total, vec(6), vec(7))
     for copy in loads[14:]:
         copy.wait()
     qres[RING - 1] = res
     to_exp2 = scale3 * (1.4426950408889634 / C**0.5)
-    for tile in (1, 0):
+
+    def queries(tile):
         for r in range(2 * tile, min(2 * tile + 2, RING - 1)):
             copy_to(kv.at[0, 0], qres.at[r], q_send.at[0], q_recv.at[r], sibling).wait_recv()
         both = qres[2 * tile : 2 * tile + 2].reshape(QT, C)
         normed = (both.astype(F32) * scale3 + shift3).astype(BF)
         q = (dot(normed, wp[0]) + vec(8)).astype(BF)
         qq[tile * QT : (tile + 1) * QT] = (dot(q, wp[1], NT) * to_exp2).astype(BF)
-        if tile == 1:
-            arrived(1)
-            arrived(2)
-            arrived(3)
+
+    queries(0)
 
     def keys(ck):
         return kv[pl.ds(2 * ck, 2)].reshape(KC, C)
@@ -403,48 +417,40 @@
             dot(p[0:POS], keys(ck)) + dot(p[POS : 2 * POS], keys(ck + 1))
         )
 
+    def score_two(r, ck, s):
+        for j in range(2):
+            s[j * POS : (j + 1) * POS] = dot(qq[r * POS : (r + 1) * POS], keys(ck + j), NT)
+
+    def soften_two(r, s, p, m, l, a):
+        step, base = 16, (r % 2) * POS
+        for i in range(0, POS, step):
+            rows, at = slice(base + i, base + i + step), slice(i, i + step)
+            low = slice(POS + i, POS + i + step)
+            sc = jnp.concatenate([s[at], s[low]], axis=1)
+            old = m[rows]
+            new = jnp.maximum(old, jnp.max(sc, axis=1, keepdims=True))
+            e = jnp.exp2(sc - jnp.concatenate([new] * (2 * KC // 128), axis=1)).astype(BF)
+            p[at] = e[:, :KC]
+            p[low] = e[:, KC:]
+            factor = jnp.exp2(old - new)
+            e32 = e.astype(F32)
+            part = l[rows] * factor
+            for j in range(2 * KC // 128):
+                part = part + e32[:, j * 128 : (j + 1) * 128]
+            l[rows] = part
+            m[rows] = new
+            a[at] = factor
+
+    def weigh_two(r, p, acc, a, ck):
+        rows = slice((r % 2) * POS, (r % 2 + 1) * POS)
+        factor = jnp.concatenate([a[0:POS]] * 4, axis=1)
+        acc[rows] = acc[rows] * factor + (
+            dot(p[0:POS], keys(ck)) + dot(p[POS : 2 * POS], keys(ck + 1))
+        )
+
     acc, m, l = (acc0, acc1), (m0, m1), (l0, l1)
     s, p, a = (s0, s1), (p0, p1), (a0, a1)
 
-    def step(b, score_of, soft_of, weigh_of):
-        if weigh_of is not None:
-            tile, ck = weigh_of
-            weigh(p[1 - b], acc[tile], a[1 - b], ck)
-        if score_of is not None:
-            score(*score_of, s[1 - b])
-        if soft_of is not None:
-            soften(s[b], p[b], m[soft_of], l[soft_of], a[b])
-
-    arrived(4)
-    ready(0)
-    score(0, 0, s0)
-    step(0, (1, 0), 0, None)
-    arrived(5)
-    arrived(6)
-    ready(1)
-    step(1, (0, 1), 1, (0, 0))
-    arrived(7)
-    arrived(8)
-    ready(2)
-    step(0, (1, 1), 0, (1, 0))
-    step(1, (0, 2), 1, (0, 1))
-    arrived(9)
-    arrived(10)
-    ready(3)
-    step(0, (1, 2), 0, (1, 1))
-    step(1, (0, 3), 1, (0, 2))
-    arrived(11)
-    arrived(12)
-    step(0, (1, 3), 0, (1, 2))
-    arrived(13)
-    arrived(14)
-    arrived(15)
-    ready(4)
-    ready(5)
-    step(1, None, 1, (0, 3))
-    score_two(1, 4, s0)
-    ready(6)
-    ready(7)
     def finish(r):
         rows = slice((r % 2) * POS, (r % 2 + 1) * POS)
         total_l = jnp.sum(l[r // 2][rows], axis=1, keepdims=True)
@@ -457,26 +463,60 @@
         ctx, lse = finish(r)
         ctx_tx[r] = ctx.astype(BF)
         lse_tx[r] = lse.T[0:8]
-        there = RING - 2 - r
-        dev = (x, y, c, ring(z, r + 1))
+        there = OWNER.index(RING - OWNER[r])
+        dev = (x, y, c, ring(z, OWNER[r]))
         sent.append(copy_to(ctx_tx.at[r], ctx_rx.at[there], c_send.at[r], c_recv.at[there], dev))
         sent.append(copy_to(lse_tx.at[r], lse_rx.at[there], e_send.at[r], e_recv.at[there], dev))
         begin(sent[-2:])
 
-    units = [(r, ck) for r in (1, 0, 2, 3) for ck in (4, 6)]
-    for u, (r, ck) in enumerate(units):
+    T, Z, O = 0, 2, 3
+    units = [
+        (T, 0), (T, 1), (Z, 0), (T, 2), (T, 3), (Z, 2), (T, 4), (T, 5),
+        (Z, 4), (O, 0), (T, 6), (Z, 6), (T, 7), (O, 2), (O, 4), (O, 6),
+    ]
+
+    def score_unit(u):
+        kind, ck = units[u]
+        score(0, ck, s[u % 2]) if kind == T else score_two(kind, ck, s[u % 2])
+
+    def weigh_unit(u):
+        kind, ck = units[u]
         b = u % 2
-        if u == 0:
-            weigh(p1, acc1, a1, 3)
+        if kind == T:
+            weigh(p[b], acc0, a[b], ck)
         else:
-            last, at = units[u - 1]
-            weigh_two(last, p[1 - b], acc[last // 2], a[1 - b], at)
+            weigh_two(kind, p[b], acc1, a[b], ck)
+
+    before = {
+        0: lambda: (arrived(5), arrived(6), ready(1)),
+        1: lambda: queries(1),
+        2: lambda: (arrived(7), ready(2)),
+        3: lambda: (arrived(8), ready(3)),
+        4: lambda: arrived(9),
+        5: lambda: (ready(4), arrived(10), arrived(11)),
+        6: lambda: ready(5),
+        8: lambda: (arrived(12), arrived(13)),
+        9: lambda: (ready(6), arrived(14), arrived(15)),
+        10: lambda: ready(7),
+    }
+    after = {12: lambda: send(2), 13: lambda: (send(0), send(1))}
+    ready(0)
+    score_unit(0)
+    for u, (kind, ck) in enumerate(units):
+        if u in before:
+            before[u]()
+        if u > 0:
+            weigh_unit(u - 1)
         if u + 1 < len(units):
-            score_two(*units[u + 1], s[1 - b])
-        soften_two(r, s[b], p[b], m[r // 2], l[r // 2], a[b])
-        if u in (2, 4, 6):
-            send(units[u - 1][0])
-    weigh_two(RING - 1, p1, acc1, a1, 6)
+            score_unit(u + 1)
+        b = u % 2
+        if kind == T:
+            soften(s[b], p[b], m0, l0, a[b])
+        else:
+            soften_two(kind, s[b], p[b], m1, l1, a[b])
+        if u in after:
+            after[u]()
+    weigh_unit(len(units) - 1)
     ctx, lse = finish(RING - 1)
     for copy in sent:
         copy.wait_recv()

time: 92.6 us -> 89.6 us (0.968)
  Pallas kernels: 90.8 us -> 87.7 us
    pallas_call x1, Pallas kernels: 90.8 us -> 87.7 us  [per_device(): pl.pallas_call(block_kernel, out_shape=jax.ShapeDtypeStruct((ROWS, COLS,...]
where the time goes in v4:
time: 89.6 us; the launch traced here: 89.4 us
  Pallas kernels  87.7 us (98%)
  local copies, waits for them, and re-layouts  1.67 us (2%)
    pallas_call x1, Pallas kernels, per_device(): pl.pallas_call(block_kernel, out_shape=jax.ShapeDtypeStruct((ROWS, COLS,...  87.7 us

profile of v4, /device:TPU:1, one launch (start us, length us, event | category | flops | bytes accessed | tf_op | source)
XLA Modules:
  0.0 89.4 jit_solution(14460586470139844299)
XLA Ops:
  0.0 87.7 %shard_map.172 = bf16[2,128,512]{2,1,0:T(8,128)(2,1)} custom-call(bf16[2,128,512]{2,1,0:T(8,128)(2,1)} %refs_0_.1, f32[1,512]{1,0:T(1,128)} %bitcast.15, f32[1,512]{1,0:T(1,128)} %bitcast.16, bf16[9,512,512]{2,1,0:T(8,128)(2,1)} %bitcast.13, f32[1,512]{1,0:T(1,128)} %bitcast.17, f32[1,512]{1,0:T(1,128)} %bitcast.18, f32[1,512]{1,0:T(1,128)} %bitcast.19, ...), custom_call_target="tpu_custom_call" | custom-call | tf_op jit(solution)/shard_map/pallas_call | solution.py:567
  87.8 1.7 %copy.20 = bf16[2,128,512]{2,1,0:T(8,128)(2,1)} copy(bf16[2,128,512]{2,1,0:T(8,128)(2,1)} %shard_map.172) | data formatting | bytes 524288

commit v5 on v4

--- a/solution.py
+++ b/solution.py
@@ -58,7 +58,7 @@
     (
         vecs, w1, w2, wp, ext, tmp, act, acc_c, hext, ar_tx, ar_rx,
         kv, qres, qq, s0, s1, p0, p1, acc0, acc1, m0, m1, l0, l1, a0, a1,
-        ctx_tx, lse_tx, ctx_rx, lse_rx,
+        ctx_tx, lse_tx, ctx_rx, lse_rx, mrg_ctx, mrg_lse,
         ld, h_send, h_recv, ar_send, ar_recv,
         kv_send, kv_recv, d_send, d_recv, q_send, q_recv, c_send, c_recv, e_send, e_recv,
     ) = refs[19:]
@@ -287,11 +287,13 @@
         (1, 1): [hand_on("y", 0, (1, 1), (1, 2)), hand_on("x", 1, (1, 1), (2, 1))],
         (3, 3): [hand_on("y", 0, (3, 3), (3, 2)), hand_on("x", 1, (3, 3), (2, 3))],
     }
-    to_z = []
-    for i in (1, 3, 2):
+    def to_column(i, h):
         place = OWNER.index(RING - i)
-        to_z.append(copy_to(kv.at[0, 0], qres.at[place], q_send.at[i - 1], q_recv.at[place],
-                            (x, y, c, ring(z, i))))
+        rows = pl.ds(h * COLS, COLS)
+        return copy_to(kv.at[0, 0, rows], qres.at[place, rows], q_send.at[place, h],
+                       q_recv.at[place, h], (x, y, c, ring(z, i)))
+
+    to_z = [to_column(i, h) for i, h in ((1, 0), (3, 0), (1, 1), (3, 1), (2, 0), (2, 1))]
     pass_own = copy_to(kv.at[0, 0], kv.at[0, 1], d_send.at[0], d_recv.at[0], sibling)
 
     def begin(copies):
@@ -312,7 +314,7 @@
     total = all_stats(
         2,
         moments(res32),
-        lambda: begin(first_x + first_y + later_x + later_y + to_z[:2]),
+        lambda: begin(first_x[:2] + first_y[:2] + later_x + later_y + first_x[2:] + first_y[2:] + to_z[:2]),
         forward,
         plane_first=True,
     )
@@ -338,10 +340,6 @@
 
     for n in range(1, 5):
         arrived(n)
-    far_half(slot_of(2, 0), 0).wait_recv()
-    far_half(slot_of(0, 2), 1).wait_recv()
-    begin(onward_two)
-
     scale3, shift3 = affine(total, vec(6), vec(7))
     for copy in loads[14:]:
         copy.wait()
@@ -350,13 +348,17 @@
 
     def queries(tile):
         for r in range(2 * tile, min(2 * tile + 2, RING - 1)):
-            copy_to(kv.at[0, 0], qres.at[r], q_send.at[0], q_recv.at[r], sibling).wait_recv()
+            for h in range(2):
+                to_column(RING - OWNER[r], h).wait_recv()
         both = qres[2 * tile : 2 * tile + 2].reshape(QT, C)
         normed = (both.astype(F32) * scale3 + shift3).astype(BF)
         q = (dot(normed, wp[0]) + vec(8)).astype(BF)
         qq[tile * QT : (tile + 1) * QT] = (dot(q, wp[1], NT) * to_exp2).astype(BF)
 
     queries(0)
+    far_half(slot_of(2, 0), 0).wait_recv()
+    far_half(slot_of(0, 2), 1).wait_recv()
+    begin(onward_two)
 
     def keys(ck):
         return kv[pl.ds(2 * ck, 2)].reshape(KC, C)
@@ -451,28 +453,65 @@
     acc, m, l = (acc0, acc1), (m0, m1), (l0, l1)
     s, p, a = (s0, s1), (p0, p1), (a0, a1)
 
-    def finish(r):
-        rows = slice((r % 2) * POS, (r % 2 + 1) * POS)
+    def finish(r, first, last):
+        rows = slice((r % 2) * POS + first, (r % 2) * POS + last)
         total_l = jnp.sum(l[r // 2][rows], axis=1, keepdims=True)
         ctx = acc[r // 2][rows] * (1.0 / total_l) * scale3 + shift3
         return ctx, m[r // 2][rows] + jnp.log2(total_l)
 
-    sent = []
-
-    def send(r):
-        ctx, lse = finish(r)
-        ctx_tx[r] = ctx.astype(BF)
-        lse_tx[r] = lse.T[0:8]
-        there = OWNER.index(RING - OWNER[r])
-        dev = (x, y, c, ring(z, OWNER[r]))
-        sent.append(copy_to(ctx_tx.at[r], ctx_rx.at[there], c_send.at[r], c_recv.at[there], dev))
-        sent.append(copy_to(lse_tx.at[r], lse_rx.at[there], e_send.at[r], e_recv.at[there], dev))
-        begin(sent[-2:])
+    def wide(v):
+        return jnp.concatenate([v] * 4, axis=1)
+
+    def received(ref):
+        return jnp.broadcast_to(ref[0:1], (COLS, COLS)).T
+
+    PIECES = (
+        (1, (mrg_ctx, mrg_lse), (0,)), (3, (mrg_ctx, mrg_lse), (1,)),
+        (1, (ctx_rx, lse_rx), (0, 1)), (3, (ctx_rx, lse_rx), (1, 0)),
+        (1, (ctx_rx, lse_rx), (0, 0)), (3, (ctx_rx, lse_rx), (1, 1)),
+    )
+
+    def piece(n):
+        dz, (ctx_to, lse_to), at = PIECES[n]
+        dev = (x, y, c, ring(z, dz))
+        return (
+            copy_to(ctx_tx.at[n], ctx_to.at[at], c_send.at[n], c_recv.at[n], dev),
+            copy_to(lse_tx.at[n], lse_to.at[at], e_send.at[n], e_recv.at[n], dev),
+        )
+
+    def send(n, ctx, lse):
+        ctx_tx[n] = ctx.astype(BF)
+        lse_tx[n] = lse.T[0:8]
+        begin(piece(n))
+
+    def arrive(n):
+        for copy in piece(n):
+            copy.wait_recv()
+
+    def send_two_away():
+        send(0, *finish(2, 0, COLS))
+        send(1, *finish(2, COLS, POS))
+
+    def send_direct():
+        send(2, *finish(0, COLS, POS))
+        send(3, *finish(1, 0, COLS))
+
+    def send_merged():
+        for n, r, first in ((0, 0, 0), (1, 1, COLS)):
+            arrive(n)
+            ctx, lse = finish(r, first, first + COLS)
+            other = received(mrg_lse[n])
+            top = jnp.maximum(lse, other)
+            one, two = jnp.exp2(lse - top), jnp.exp2(other - top)
+            both = one + two
+            inv = 1.0 / both
+            send(4 + n, ctx * wide(one * inv) + mrg_ctx[n].astype(F32) * wide(two * inv),
+                 top + jnp.log2(both))
 
     T, Z, O = 0, 2, 3
     units = [
         (T, 0), (T, 1), (Z, 0), (T, 2), (T, 3), (Z, 2), (T, 4), (T, 5),
-        (Z, 4), (O, 0), (T, 6), (Z, 6), (T, 7), (O, 2), (O, 4), (O, 6),
+        (Z, 4), (Z, 6), (T, 6), (T, 7), (O, 0), (O, 2), (O, 4), (O, 6),
     ]
 
     def score_unit(u):
@@ -488,18 +527,17 @@
             weigh_two(kind, p[b], acc1, a[b], ck)
 
     before = {
-        0: lambda: (arrived(5), arrived(6), ready(1)),
-        1: lambda: queries(1),
+        0: lambda: ready(1),
+        1: lambda: (arrived(5), arrived(6), queries(1)),
         2: lambda: (arrived(7), ready(2)),
-        3: lambda: (arrived(8), ready(3)),
-        4: lambda: arrived(9),
+        3: lambda: ready(3),
+        4: lambda: (arrived(8), arrived(9)),
         5: lambda: (ready(4), arrived(10), arrived(11)),
         6: lambda: ready(5),
-        8: lambda: (arrived(12), arrived(13)),
-        9: lambda: (ready(6), arrived(14), arrived(15)),
-        10: lambda: ready(7),
+        7: lambda: (arrived(12), arrived(13), arrived(14), arrived(15)),
+        8: lambda: (ready(6), ready(7)),
     }
-    after = {12: lambda: send(2), 13: lambda: (send(0), send(1))}
+    after = {10: send_two_away, 12: send_direct, 13: send_merged}
     ready(0)
     score_unit(0)
     for u, (kind, ck) in enumerate(units):
@@ -517,29 +555,31 @@
         if u in after:
             after[u]()
     weigh_unit(len(units) - 1)
-    ctx, lse = finish(RING - 1)
-    for copy in sent:
-        copy.wait_recv()
-    others = [jnp.broadcast_to(lse_rx[r, 0:1], (128, POS)).T for r in range(RING - 1)]
-    top = lse
-    for o in others:
-        top = jnp.maximum(top, o)
+    ctx, lse = finish(RING - 1, 0, POS)
+    for n in range(2, 6):
+        arrive(n)
+    others = [
+        jnp.concatenate([received(lse_rx[f, h]) for h in range(2)], axis=0) for f in range(2)
+    ]
+    top = jnp.maximum(jnp.maximum(lse, others[0]), others[1])
     weight = jnp.exp2(lse - top)
     norm = weight
-    ctx = ctx * jnp.concatenate([weight] * 4, axis=1)
-    for r, o in enumerate(others):
+    ctx = ctx * wide(weight)
+    for f, o in enumerate(others):
         w = jnp.exp2(o - top)
         norm = norm + w
-        ctx = ctx + ctx_rx[r].astype(F32) * jnp.concatenate([w] * 4, axis=1)
-    inv = 1.0 / norm
-    ctx = (ctx * jnp.concatenate([inv] * 4, axis=1)).astype(BF)
+        ctx = ctx + ctx_rx[f].reshape(POS, C).astype(F32) * wide(w)
+    ctx = (ctx * wide(1.0 / norm)).astype(BF)
     attended = (dot(ctx, wp[2]) + vec(9)).astype(BF)
     mixed = qres[RING - 1].astype(F32) + dot(attended, wp[3]) + vec(10)
     out[...] = mixed.astype(BF).reshape(ROWS, COLS, C)
-    for copy in halo0 + halo1 + first_x + first_y + later_x + later_y + moved + to_z + sent:
+    for copy in halo0 + halo1 + first_x + first_y + later_x + later_y + moved + to_z:
         copy.wait_send()
     for n in range(SLOTS):
         pass_on(n).wait_send()
+    for n in range(6):
+        for copy in piece(n):
+            copy.wait_send()
 
 
 def per_device(latent, *params):
@@ -559,10 +599,11 @@
         v((QT, C), F32), v((QT, C), F32),
         v((QT, 128), F32), v((QT, 128), F32), v((QT, 128), F32), v((QT, 128), F32),
         v((QT, 128), F32), v((QT, 128), F32),
-        v((3, POS, C), BF), v((3, 8, POS), F32), v((3, POS, C), BF), v((3, 8, POS), F32),
+        v((6, COLS, C), BF), v((6, 8, COLS), F32), v((2, 2, COLS, C), BF), v((2, 2, 8, COLS), F32),
+        v((2, COLS, C), BF), v((2, 8, COLS), F32),
         dma((18,)), dma((2, 8)), dma((2, 8)), dma((3, 22)), dma((3, 22)),
-        dma((30,)), dma((SLOTS, 2)), dma((SLOTS,)), dma((SLOTS,)), dma((3,)), dma((3,)),
-        dma((3,)), dma((3,)), dma((3,)), dma((3,)),
+        dma((30,)), dma((SLOTS, 2)), dma((SLOTS,)), dma((SLOTS,)), dma((3, 2)), dma((3, 2)),
+        dma((6,)), dma((6,)), dma((6,)), dma((6,)),
     ]
     return pl.pallas_call(
         block_kernel,

time: 89.6 us -> 82.8 us (0.924)
  Pallas kernels: 87.7 us -> 81 us
    pallas_call x1, Pallas kernels: 87.7 us -> 81 us  [per_device(): pl.pallas_call(block_kernel, out_shape=jax.ShapeDtypeStruct((ROWS, COLS,...]
where the time goes in v5:
time: 82.8 us; the launch traced here: 82.7 us
  Pallas kernels  81 us (98%)
  local copies, waits for them, and re-layouts  1.67 us (2%)
    pallas_call x1, Pallas kernels, per_device(): pl.pallas_call(block_kernel, out_shape=jax.ShapeDtypeStruct((ROWS, COLS,...  81 us
    unnamed x1, local copies, waits for them, and re-layouts  1.67 us

profile of v5, /device:TPU:1, one launch (start us, length us, event | category | flops | bytes accessed | tf_op | source)
XLA Modules:
  0.0 82.7 jit_solution(18037528232110843532)
XLA Ops:
  0.0 81.0 %shard_map.172 = bf16[2,128,512]{2,1,0:T(8,128)(2,1)} custom-call(bf16[2,128,512]{2,1,0:T(8,128)(2,1)} %refs_0_.1, f32[1,512]{1,0:T(1,128)} %bitcast.15, f32[1,512]{1,0:T(1,128)} %bitcast.16, bf16[9,512,512]{2,1,0:T(8,128)(2,1)} %bitcast.13, f32[1,512]{1,0:T(1,128)} %bitcast.17, f32[1,512]{1,0:T(1,128)} %bitcast.18, f32[1,512]{1,0:T(1,128)} %bitcast.19, ...), custom_call_target="tpu_custom_call" | custom-call | tf_op jit(solution)/shard_map/pallas_call | solution.py:608
  81.0 1.7 %copy.20 = bf16[2,128,512]{2,1,0:T(8,128)(2,1)} copy(bf16[2,128,512]{2,1,0:T(8,128)(2,1)} %shard_map.172) | data formatting | bytes 524288

commit v6 on v5

--- a/solution.py
+++ b/solution.py
@@ -56,7 +56,7 @@
     hbm = refs[:18]
     out = refs[18]
     (
-        vecs, w1, w2, wp, ext, tmp, act, acc_c, hext, ar_tx, ar_rx,
+        vecs, w1, w2, wp, ext, tmp, act, hext, ar_tx, ar_rx,
         kv, qres, qq, s0, s1, p0, p1, acc0, acc1, m0, m1, l0, l1, a0, a1,
         ctx_tx, lse_tx, ctx_rx, lse_rx, mrg_ctx, mrg_lse,
         ld, h_send, h_recv, ar_send, ar_recv,
@@ -184,30 +184,25 @@
         col = lax.broadcasted_iota(jnp.int32, (width, 1), 0)
         edge = ((col >= pad) | (z > 0)) & ((col < pad + COLS) | (z < RING - 1))
 
-        def one_row(r, _):
-            inside = ((r > 0) | (t > 0)) & ((r < 3) | (t < TILES - 1))
+        for r in range(4):
+            inside = edge
+            if r == 0:
+                inside = edge & (t > 0)
+            if r == 3:
+                inside = edge & (t < TILES - 1)
             u = buf[r].astype(F32) * scale + shift
             u = u / (1.0 + jnp.exp(-u))
-            tmp[0:width] = jnp.where(edge & inside, u, 0.0)
+            tmp[r, 0:width] = jnp.where(inside, u, 0.0)
             for dj in range(3):
-                act[dj, r] = tmp[pad - 1 + dj : pad - 1 + dj + COLS].astype(BF)
-            return 0
-
-        lax.fori_loop(0, 4, one_row, 0)
+                act[dj, r] = tmp[r, pad - 1 + dj : pad - 1 + dj + COLS].astype(BF)
 
     def conv(weight):
-        acc_c[...] = jnp.zeros_like(acc_c)
-
-        def three_taps(di, _):
-            part = None
+        total = None
+        for di in range(3):
             for dj in range(3):
-                a = act[dj, pl.ds(di, 2)].reshape(POS, C)
-                d = dot(a, weight[di * 3 + dj])
-                part = d if part is None else part + d
-            acc_c[...] += part
-            return 0
-
-        lax.fori_loop(0, 3, three_taps, 0)
+                d = dot(act[dj, di : di + 2].reshape(POS, C), weight[di * 3 + dj])
+                total = d if total is None else total + d
+        return total
 
     def vec(i):
         return vecs[i]
@@ -227,9 +222,8 @@
     scale, shift = affine(total, vec(0), vec(1))
     activate(ext, LPAD, COLS + 2 * LPAD, scale, shift)
     loads[12].wait()
-    conv(w1)
-
-    hid = acc_c[...] + vec(2)
+    hid = conv(w1) + vec(2)
+
     hext[1:3, HPAD : HPAD + COLS] = hid.reshape(ROWS, COLS, C)
     halo1 = halo(hext, HPAD, 1)
 
@@ -243,9 +237,9 @@
     scale, shift = affine(total, vec(3), vec(4))
     activate(hext, HPAD, COLS + 2 * HPAD, scale, shift)
     loads[13].wait()
-    conv(w2)
+    second = conv(w2) + vec(5)
     latent = ext[1:3, LPAD : LPAD + COLS].astype(F32).reshape(POS, C)
-    res = (latent + (acc_c[...] + vec(5))).astype(BF)
+    res = (latent + second).astype(BF)
     kv[0, 0] = res
 
     def half(n, h):
@@ -373,13 +367,12 @@
             sc = s[rows]
             old = m[rows]
             new = jnp.maximum(old, jnp.max(sc, axis=1, keepdims=True))
-            e = jnp.exp2(sc - jnp.concatenate([new] * (KC // 128), axis=1)).astype(BF)
-            p[rows] = e
+            e = jnp.exp2(sc - jnp.concatenate([new] * (KC // 128), axis=1))
+            p[rows] = e.astype(BF)
             factor = jnp.exp2(old - new)
-            e32 = e.astype(F32)
             part = l[rows] * factor
             for j in range(KC // 128):
-                part = part + e32[:, j * 128 : (j + 1) * 128]
+                part = part + e[:, j * 128 : (j + 1) * 128]
             l[rows] = part
             m[rows] = new
             a[rows] = factor
@@ -400,45 +393,13 @@
             sc = jnp.concatenate([s[at], s[low]], axis=1)
             old = m[rows]
             new = jnp.maximum(old, jnp.max(sc, axis=1, keepdims=True))
-            e = jnp.exp2(sc - jnp.concatenate([new] * (2 * KC // 128), axis=1)).astype(BF)
-            p[at] = e[:, :KC]
-            p[low] = e[:, KC:]
+            e = jnp.exp2(sc - jnp.concatenate([new] * (2 * KC // 128), axis=1))
+            p[at] = e[:, :KC].astype(BF)
+            p[low] = e[:, KC:].astype(BF)
             factor = jnp.exp2(old - new)
-            e32 = e.astype(F32)
             part = l[rows] * factor
             for j in range(2 * KC // 128):
-                part = part + e32[:, j * 128 : (j + 1) * 128]
-            l[rows] = part
-            m[rows] = new
-            a[at] = factor
-
-    def weigh_two(r, p, acc, a, ck):
-        rows = slice((r % 2) * POS, (r % 2 + 1) * POS)
-        factor = jnp.concatenate([a[0:POS]] * 4, axis=1)
-        acc[rows] = acc[rows] * factor + (
-            dot(p[0:POS], keys(ck)) + dot(p[POS : 2 * POS], keys(ck + 1))
-        )
-
-    def score_two(r, ck, s):
-        for j in range(2):
-            s[j * POS : (j + 1) * POS] = dot(qq[r * POS : (r + 1) * POS], keys(ck + j), NT)
-
-    def soften_two(r, s, p, m, l, a):
-        step, base = 16, (r % 2) * POS
-        for i in range(0, POS, step):
-            rows, at = slice(base + i, base + i + step), slice(i, i + step)
-            low = slice(POS + i, POS + i + step)
-            sc = jnp.concatenate([s[at], s[low]], axis=1)
-            old = m[rows]
-            new = jnp.maximum(old, jnp.max(sc, axis=1, keepdims=True))
-            e = jnp.exp2(sc - jnp.concatenate([new] * (2 * KC // 128), axis=1)).astype(BF)
-            p[at] = e[:, :KC]
-            p[low] = e[:, KC:]
-            factor = jnp.exp2(old - new)
-            e32 = e.astype(F32)
-            part = l[rows] * factor
-            for j in range(2 * KC // 128):
-                part = part + e32[:, j * 128 : (j + 1) * 128]
+                part = part + e[:, j * 128 : (j + 1) * 128]
             l[rows] = part
             m[rows] = new
             a[at] = factor
@@ -591,8 +552,8 @@
     v = pltpu.VMEM
     scratch = [
         v((11, 1, C), F32), v((9, C, C), BF), v((9, C, C), BF), v((4, C, C), BF),
-        v((4, COLS + 2 * LPAD, C), BF), v((COLS + 2 * LPAD, C), F32), v((3, 4, COLS, C), BF),
-        v((POS, C), F32), v((4, COLS + 2 * HPAD, C), F32),
+        v((4, COLS + 2 * LPAD, C), BF), v((4, COLS + 2 * LPAD, C), F32), v((3, 4, COLS, C), BF),
+        v((4, COLS + 2 * HPAD, C), F32),
         v((3, 2, 2, C), F32), v((3, 22, 2, C), F32),
         v((SLOTS, 2, POS, C), BF), v((RING, POS, C), BF), v((RING * POS, C), BF),
         v((QT, KC), F32), v((QT, KC), F32), v((QT, KC), BF), v((QT, KC), BF),

time: 82.8 us -> 81 us (0.978)
  Pallas kernels: 81 us -> 79.2 us
    pallas_call x1, Pallas kernels: 81 us -> 79.2 us  [per_device(): pl.pallas_call(block_kernel, out_shape=jax.ShapeDtypeStruct((ROWS, COLS,...]
where the time goes in v6:
time: 81 us; the launch traced here: 80.8 us
  Pallas kernels  79.2 us (98%)
  local copies, waits for them, and re-layouts  1.67 us (2%)
    pallas_call x1, Pallas kernels, per_device(): pl.pallas_call(block_kernel, out_shape=jax.ShapeDtypeStruct((ROWS, COLS,...  79.2 us
    unnamed x1, local copies, waits for them, and re-layouts  1.67 us

profile of v6, /device:TPU:1, one launch (start us, length us, event | category | flops | bytes accessed | tf_op | source)
XLA Modules:
  0.0 80.8 jit_solution(7270825347642838887)
XLA Ops:
  0.0 79.2 %shard_map.172 = bf16[2,128,512]{2,1,0:T(8,128)(2,1)} custom-call(bf16[2,128,512]{2,1,0:T(8,128)(2,1)} %refs_0_.1, f32[1,512]{1,0:T(1,128)} %bitcast.15, f32[1,512]{1,0:T(1,128)} %bitcast.16, bf16[9,512,512]{2,1,0:T(8,128)(2,1)} %bitcast.13, f32[1,512]{1,0:T(1,128)} %bitcast.17, f32[1,512]{1,0:T(1,128)} %bitcast.18, f32[1,512]{1,0:T(1,128)} %bitcast.19, ...), custom_call_target="tpu_custom_call" | custom-call | tf_op jit(solution)/shard_map/pallas_call | solution.py:569
  79.2 1.7 %copy.20 = bf16[2,128,512]{2,1,0:T(8,128)(2,1)} copy(bf16[2,128,512]{2,1,0:T(8,128)(2,1)} %shard_map.172) | data formatting | bytes 524288

commit v7 on v6

--- a/solution.py
+++ b/solution.py
@@ -137,9 +137,19 @@
             )
         return copies
 
+    lane = lax.broadcasted_iota(jnp.int32, (8, 128), 1)
+    mine = lax.rem(lane, 16) == lax.broadcasted_iota(jnp.int32, (8, 128), 0)
+
+    def over_groups(v):
+        for d in (1, 2, 4, 8):
+            v = v + jnp.where((lane & d) == 0, pltpu.roll(v, 128 - d, 1), pltpu.roll(v, d, 1))
+        return v
+
     def moments(v):
-        return jnp.concatenate(
-            [jnp.sum(v, axis=0, keepdims=True), jnp.sum(v * v, axis=0, keepdims=True)], axis=0
+        both = (jnp.sum(v, axis=0, keepdims=True), jnp.sum(v * v, axis=0, keepdims=True))
+        rows = [b[:, n * 128 : (n + 1) * 128] for b in both for n in range(4)]
+        return jnp.sum(
+            jnp.where(mine, over_groups(jnp.concatenate(rows, axis=0)), 0.0), axis=0, keepdims=True
         )
 
     def all_stats(k, local, after_first, after_second, plane_first=False):
@@ -166,17 +176,14 @@
             copy.wait_send()
         return total
 
-    lane = lax.broadcasted_iota(jnp.int32, (8, C), 1)
-
     def affine(total, gain, shift):
-        both = jnp.concatenate([total, jnp.zeros((6, C), F32)], axis=0)
-        for d in (1, 2, 4, 8):
-            up = pltpu.roll(both, C - d, 1)
-            down = pltpu.roll(both, d, 1)
-            both = both + jnp.where((lane & d) == 0, up, down)
+        rows = over_groups(jnp.where(mine, jnp.broadcast_to(total, (8, 128)), 0.0))
+        sums, squares = (
+            jnp.concatenate([rows[n : n + 1] for n in range(k, k + 4)], axis=1) for k in (0, 4)
+        )
         members = float(POS * TILES * RING * (C // GROUPS))
-        mean = both[0:1] / members
-        var = jnp.maximum(both[1:2] / members - mean * mean, 0.0)
+        mean = sums / members
+        var = jnp.maximum(squares / members - mean * mean, 0.0)
         scale = lax.rsqrt(var + EPS) * gain
         return scale, shift - mean * scale
 
@@ -257,12 +264,13 @@
     later_y = [own_copy("y", i, 0, 8 + k) for k, i in enumerate((1, 3))]
     moved = []
 
-    def hand_on(axis, h, source, there):
+    def hand_on(axis, h, source, there, first=0, rows=COLS):
         step = (source[0] - there[0], source[1] - there[1])
         dev = (ring(x, step[0] % RING), y, c, z) if axis == "x" else (x, ring(y, step[1] % RING), c, z)
         n = slot_of(*there)
-        copy = copy_to(half(slot_of(*source), h), half(n, h), kv_send.at[10 + len(moved)],
-                       kv_recv.at[n, h], dev)
+        part = pl.ds(h * COLS + first, rows)
+        copy = copy_to(kv.at[slot_of(*source), 0, part], kv.at[n, 0, part],
+                       kv_send.at[10 + len(moved)], kv_recv.at[n, h], dev)
         moved.append(copy)
         return copy
 
@@ -276,8 +284,10 @@
         onward_two.append(hand_on("y", 0, (2, 0), (2, k)))
         onward_two.append(hand_on("x", 1, (0, 2), (k, 2)))
     relays = {
-        (1, 0): [hand_on("x", 1, (1, 0), (2, 0))],
-        (0, 1): [hand_on("y", 0, (0, 1), (0, 2))],
+        (1, 0): [hand_on("x", 1, (1, 0), (2, 0), 0, 64)],
+        (3, 0): [hand_on("x", 1, (3, 0), (2, 0), 64, 64)],
+        (0, 1): [hand_on("y", 0, (0, 1), (0, 2), 0, 64)],
+        (0, 3): [hand_on("y", 0, (0, 3), (0, 2), 64, 64)],
         (1, 1): [hand_on("y", 0, (1, 1), (1, 2)), hand_on("x", 1, (1, 1), (2, 1))],
         (3, 3): [hand_on("y", 0, (3, 3), (3, 2)), hand_on("x", 1, (3, 3), (2, 3))],
     }
@@ -554,7 +564,7 @@
         v((11, 1, C), F32), v((9, C, C), BF), v((9, C, C), BF), v((4, C, C), BF),
         v((4, COLS + 2 * LPAD, C), BF), v((4, COLS + 2 * LPAD, C), F32), v((3, 4, COLS, C), BF),
         v((4, COLS + 2 * HPAD, C), F32),
-        v((3, 2, 2, C), F32), v((3, 22, 2, C), F32),
+        v((3, 2, 1, 128), F32), v((3, 22, 1, 128), F32),
         v((SLOTS, 2, POS, C), BF), v((RING, POS, C), BF), v((RING * POS, C), BF),
         v((QT, KC), F32), v((QT, KC), F32), v((QT, KC), BF), v((QT, KC), BF),
         v((QT, C), F32), v((QT, C), F32),
@@ -563,7 +573,7 @@
         v((6, COLS, C), BF), v((6, 8, COLS), F32), v((2, 2, COLS, C), BF), v((2, 2, 8, COLS), F32),
         v((2, COLS, C), BF), v((2, 8, COLS), F32),
         dma((18,)), dma((2, 8)), dma((2, 8)), dma((3, 22)), dma((3, 22)),
-        dma((30,)), dma((SLOTS, 2)), dma((SLOTS,)), dma((SLOTS,)), dma((3, 2)), dma((3, 2)),
+        dma((32,)), dma((SLOTS, 2)), dma((SLOTS,)), dma((SLOTS,)), dma((3, 2)), dma((3, 2)),
         dma((6,)), dma((6,)), dma((6,)), dma((6,)),
     ]
     return pl.pallas_call(

time: 81 us -> 78.4 us (0.968)
  Pallas kernels: 79.2 us -> 76.6 us
    pallas_call x1, Pallas kernels: 79.2 us -> 76.6 us  [per_device(): pl.pallas_call(block_kernel, out_shape=jax.ShapeDtypeStruct((ROWS, COLS,...]
where the time goes in v7:
time: 78.4 us; the launch traced here: 78.3 us
  Pallas kernels  76.6 us (98%)
  local copies, waits for them, and re-layouts  1.67 us (2%)
    pallas_call x1, Pallas kernels, per_device(): pl.pallas_call(block_kernel, out_shape=jax.ShapeDtypeStruct((ROWS, COLS,...  76.6 us
    unnamed x1, local copies, waits for them, and re-layouts  1.67 us

profile of v7, /device:TPU:1, one launch (start us, length us, event | category | flops | bytes accessed | tf_op | source)
XLA Modules:
  0.0 78.3 jit_solution(9135125252839617701)
XLA Ops:
  0.0 76.6 %shard_map.172 = bf16[2,128,512]{2,1,0:T(8,128)(2,1)} custom-call(bf16[2,128,512]{2,1,0:T(8,128)(2,1)} %refs_0_.1, f32[1,512]{1,0:T(1,128)} %bitcast.15, f32[1,512]{1,0:T(1,128)} %bitcast.16, bf16[9,512,512]{2,1,0:T(8,128)(2,1)} %bitcast.13, f32[1,512]{1,0:T(1,128)} %bitcast.17, f32[1,512]{1,0:T(1,128)} %bitcast.18, f32[1,512]{1,0:T(1,128)} %bitcast.19, ...), custom_call_target="tpu_custom_call" | custom-call | tf_op jit(solution)/shard_map/pallas_call | solution.py:579
  76.6 1.7 %copy.20 = bf16[2,128,512]{2,1,0:T(8,128)(2,1)} copy(bf16[2,128,512]{2,1,0:T(8,128)(2,1)} %shard_map.172) | data formatting | bytes 524288

commit v8 on v7

--- a/solution.py
+++ b/solution.py
@@ -85,15 +85,7 @@
     loads.append(pltpu.make_async_copy(cw2, w2, ld.at[13]))
     for i, w in enumerate((wq, wk, wv, wo)):
         loads.append(pltpu.make_async_copy(w, wp.at[i], ld.at[14 + i]))
-    for copy in loads:
-        copy.start()
-
-    for ref in (acc0, acc1, l0, l1):
-        ref[...] = jnp.zeros_like(ref)
-    for ref in (m0, m1):
-        ref[...] = jnp.full_like(ref, -1e30)
-    a1[...] = jnp.ones_like(a1)
-    p1[...] = jnp.zeros_like(p1)
+    loads[0].start()
 
     barrier = pltpu.get_barrier_semaphore()
     column = [sibling]
@@ -108,7 +100,15 @@
             peers.append(tile_dev(dt, dz))
     for dev in peers:
         pl.semaphore_signal(barrier, inc=1, device_id=dev, device_id_type=MESH)
-    pl.semaphore_wait(barrier, len(peers))
+    for copy in loads[1:]:
+        copy.start()
+
+    for ref in (acc0, acc1, l0, l1):
+        ref[...] = jnp.zeros_like(ref)
+    for ref in (m0, m1):
+        ref[...] = jnp.full_like(ref, -1e30)
+    a1[...] = jnp.ones_like(a1)
+    p1[...] = jnp.zeros_like(p1)
 
     loads[0].wait()
 
@@ -152,9 +152,10 @@
             jnp.where(mine, over_groups(jnp.concatenate(rows, axis=0)), 0.0), axis=0, keepdims=True
         )
 
+    stats_sent = []
+
     def all_stats(k, local, after_first, after_second, plane_first=False):
         total = local
-        pending = []
         stages = [(0, column), (len(column), plane)]
         if plane_first:
             stages.reverse()
@@ -171,9 +172,7 @@
             for n, copy in enumerate(copies):
                 copy.wait_recv()
                 total = total + ar_rx[k, base + n]
-            pending += copies
-        for copy in pending:
-            copy.wait_send()
+            stats_sent.extend(copies)
         return total
 
     def affine(total, gain, shift):
@@ -221,7 +220,9 @@
         for copy in halo0:
             copy.start()
 
-    total = all_stats(0, moments(latent), start_halo0, lambda: None)
+    first_moments = moments(latent)
+    pl.semaphore_wait(barrier, len(peers))
+    total = all_stats(0, first_moments, start_halo0, lambda: None)
     for copy in loads[1:12]:
         copy.wait()
     for copy in halo0:
@@ -508,7 +509,8 @@
         7: lambda: (arrived(12), arrived(13), arrived(14), arrived(15)),
         8: lambda: (ready(6), ready(7)),
     }
-    after = {10: send_two_away, 12: send_direct, 13: send_merged}
+    leave = {10: send_two_away, 12: send_direct}
+    after = {13: send_merged}
     ready(0)
     score_unit(0)
     for u, (kind, ck) in enumerate(units):
@@ -516,6 +518,8 @@
             before[u]()
         if u > 0:
             weigh_unit(u - 1)
+        if u in leave:
+            leave[u]()
         if u + 1 < len(units):
             score_unit(u + 1)
         b = u % 2
@@ -527,6 +531,10 @@
             after[u]()
     weigh_unit(len(units) - 1)
     ctx, lse = finish(RING - 1, 0, POS)
+    for copy in stats_sent + halo0 + halo1 + first_x + first_y + later_x + later_y + moved + to_z:
+        copy.wait_send()
+    for n in range(SLOTS):
+        pass_on(n).wait_send()
     for n in range(2, 6):
         arrive(n)
     others = [
@@ -544,10 +552,6 @@
     attended = (dot(ctx, wp[2]) + vec(9)).astype(BF)
     mixed = qres[RING - 1].astype(F32) + dot(attended, wp[3]) + vec(10)
     out[...] = mixed.astype(BF).reshape(ROWS, COLS, C)
-    for copy in halo0 + halo1 + first_x + first_y + later_x + later_y + moved + to_z:
-        copy.wait_send()
-    for n in range(SLOTS):
-        pass_on(n).wait_send()
     for n in range(6):
         for copy in piece(n):
             copy.wait_send()

time: 78.4 us -> 77.8 us (level)
  no operation moved by 1% of the time
where the time goes in v8:
time: 77.8 us; the launch traced here: 77.6 us
  Pallas kernels  76 us (98%)
  local copies, waits for them, and re-layouts  1.67 us (2%)
    pallas_call x1, Pallas kernels, per_device(): pl.pallas_call(block_kernel, out_shape=jax.ShapeDtypeStruct((ROWS, COLS,...  76 us
    unnamed x1, local copies, waits for them, and re-layouts  1.67 us

profile of v8, /device:TPU:1, one launch (start us, length us, event | category | flops | bytes accessed | tf_op | source)
XLA Modules:
  0.0 77.6 jit_solution(9020469334667812697)
XLA Ops:
  0.0 76.0 %shard_map.172 = bf16[2,128,512]{2,1,0:T(8,128)(2,1)} custom-call(bf16[2,128,512]{2,1,0:T(8,128)(2,1)} %refs_0_.1, f32[1,512]{1,0:T(1,128)} %bitcast.15, f32[1,512]{1,0:T(1,128)} %bitcast.16, bf16[9,512,512]{2,1,0:T(8,128)(2,1)} %bitcast.13, f32[1,512]{1,0:T(1,128)} %bitcast.17, f32[1,512]{1,0:T(1,128)} %bitcast.18, f32[1,512]{1,0:T(1,128)} %bitcast.19, ...), custom_call_target="tpu_custom_call" | custom-call | tf_op jit(solution)/shard_map/pallas_call | solution.py:583
  76.0 1.7 %copy.20 = bf16[2,128,512]{2,1,0:T(8,128)(2,1)} copy(bf16[2,128,512]{2,1,0:T(8,128)(2,1)} %shard_map.172) | data formatting | bytes 524288

commit v9 on v8

--- a/solution.py
+++ b/solution.py
@@ -514,12 +514,12 @@
     ready(0)
     score_unit(0)
     for u, (kind, ck) in enumerate(units):
-        if u in before:
-            before[u]()
         if u > 0:
             weigh_unit(u - 1)
         if u in leave:
             leave[u]()
+        if u in before:
+            before[u]()
         if u + 1 < len(units):
             score_unit(u + 1)
         b = u % 2

time: 77.8 us -> 77.6 us (level)
  no operation moved by 1% of the time
where the time goes in v9:
time: 77.6 us; the launch traced here: 77.4 us
  Pallas kernels  75.8 us (98%)
  local copies, waits for them, and re-layouts  1.67 us (2%)
    pallas_call x1, Pallas kernels, per_device(): pl.pallas_call(block_kernel, out_shape=jax.ShapeDtypeStruct((ROWS, COLS,...  75.8 us
    unnamed x1, local copies, waits for them, and re-layouts  1.67 us

profile of v9, /device:TPU:1, one launch (start us, length us, event | category | flops | bytes accessed | tf_op | source)
XLA Modules:
  0.0 77.4 jit_solution(14097573055932443090)
XLA Ops:
  0.0 75.8 %shard_map.172 = bf16[2,128,512]{2,1,0:T(8,128)(2,1)} custom-call(bf16[2,128,512]{2,1,0:T(8,128)(2,1)} %refs_0_.1, f32[1,512]{1,0:T(1,128)} %bitcast.15, f32[1,512]{1,0:T(1,128)} %bitcast.16, bf16[9,512,512]{2,1,0:T(8,128)(2,1)} %bitcast.13, f32[1,512]{1,0:T(1,128)} %bitcast.17, f32[1,512]{1,0:T(1,128)} %bitcast.18, f32[1,512]{1,0:T(1,128)} %bitcast.19, ...), custom_call_target="tpu_custom_call" | custom-call | tf_op jit(solution)/shard_map/pallas_call | solution.py:583
  75.8 1.7 %copy.20 = bf16[2,128,512]{2,1,0:T(8,128)(2,1)} copy(bf16[2,128,512]{2,1,0:T(8,128)(2,1)} %shard_map.172) | data formatting | bytes 524288
